TPU v7x, 8 devices: a whole 2x2x1 slice. The times are simulated.
8 devices in a mesh: data: 1 (over z), pp: 2 (over y), ep: 4 (over x, core).
Axes of the slice: x: 2, y: 2, z: 1, core: 2. Of those that a mesh axis runs over, the one named last changes fastest.
Arguments:
- expert_out: bfloat16 [2, 1, 384, 32, 7168], P(('data', 'pp'), None, 'ep')
- expert_id: int32 [2, 1, 1024, 8], P(('data', 'pp'), None, 'ep')
- slot_id: int32 [2, 1, 1024, 8], P(('data', 'pp'), None, 'ep')
- gate: float32 [2, 1, 1024, 8], P(('data', 'pp'), None, 'ep')
- resid: bfloat16 [2, 1, 1024, 7168], P(('data', 'pp'), None, 'ep')
- owner: int32 [2, 32], P(('data', 'pp'))
- norm_w: float32 [2, 7168], P('pp')
- w_q: bfloat16 [2, 7168, 8192], P('pp')
- w_k: bfloat16 [2, 7168, 8192], P('pp')
- w_v: bfloat16 [2, 7168, 8192], P('pp')
- w_o: bfloat16 [2, 8192, 7168], P('pp')
Outputs:
- output: bfloat16 [2, 1, 1024, 7168], P(('data', 'pp'), None, 'ep')
All inputs are finite; a program needn't handle non-finite values.
Results may differ from a plain program's by a relative error of at most 0.013573.
Values are sent between devices in bfloat16 or wider.
A program may use at most 2 GiB of HBM per device.

v0:
```python
import jax
import jax.numpy as jnp
from jax import lax
from jax.sharding import PartitionSpec as P

HEAD_DIM = 128
NORM_EPS = 1e-6


def attend_local(y_owned, norm_scale, w_q, w_k, w_v, w_o):
    n_micro, n_seqs, seq_len, model_dim = y_owned.shape
    n_heads = w_q.shape[1] // HEAD_DIM
    y_f32 = y_owned.astype(jnp.float32)
    inv_rms = lax.rsqrt(jnp.mean(y_f32 * y_f32, axis=-1, keepdims=True) + NORM_EPS)
    normed = (y_f32 * inv_rms * norm_scale).astype(jnp.bfloat16)

    def project(weight):
        proj_out = jnp.einsum('msld,de->msle', normed, weight, preferred_element_type=jnp.float32)
        return proj_out.astype(jnp.bfloat16).reshape(n_micro, n_seqs, seq_len, n_heads, HEAD_DIM)

    queries = project(w_q)
    key_vecs = project(w_k)
    values = project(w_v)
    scores = jnp.einsum('msqhe,mskhe->mshqk', queries, key_vecs, preferred_element_type=jnp.float32) * (HEAD_DIM ** -0.5)
    causal = jnp.arange(seq_len)[:, None] >= jnp.arange(seq_len)[None, :]
    attn_probs = jax.nn.softmax(jnp.where(causal, scores, -1e30), axis=-1).astype(jnp.bfloat16)
    head_mix = jnp.einsum('mshqk,mskhe->msqhe', attn_probs, values, preferred_element_type=jnp.float32).astype(jnp.bfloat16)
    out_proj = jnp.einsum('msqhe,hed->msqd', head_mix, w_o.reshape(n_heads, HEAD_DIM, model_dim), preferred_element_type=jnp.float32)
    return (y_f32 + out_proj.astype(jnp.bfloat16).astype(jnp.float32)).astype(jnp.bfloat16)


def combine_home(recv_out, expert_id, slot_id, gate, resid, dev_index, cap_dev):
    n_micro = recv_out.shape[0]
    model_dim = recv_out.shape[3]
    kept_mask = slot_id >= 0
    local_slot = jnp.where(kept_mask, slot_id - dev_index * cap_dev, 0)
    row_index = expert_id * cap_dev + local_slot
    flat_out = recv_out.reshape(n_micro, -1, model_dim)
    picked = jax.vmap(lambda out_table, row_ids: out_table[row_ids])(flat_out, row_index)
    weights = jnp.where(kept_mask, gate, 0.0)
    combined = jnp.sum(picked.astype(jnp.float32) * weights[..., None], axis=2)
    return (resid.astype(jnp.float32) + combined).astype(jnp.bfloat16)


def solution(mesh):
    n_stages = mesh.shape['pp']
    n_ep = mesh.shape['ep']
    next_rank = [(src_rank, (src_rank + 1) % n_stages) for src_rank in range(n_stages)]
    group_axes = ('data', 'pp')

    def device_step(expert_out, expert_id, slot_id, gate, resid, owner, norm_w, w_q, w_k, w_v, w_o):
        dev_index = lax.axis_index('ep')
        out_local = expert_out[0]
        cap_dev = out_local.shape[2] // n_ep
        recv_out = lax.all_to_all(out_local, 'ep', 2, 1, tiled=True)
        y_home = combine_home(recv_out, expert_id[0], slot_id[0], gate[0], resid[0], dev_index, cap_dev)
        y_next = lax.ppermute(y_home, 'pp', next_rank)
        n_micro, tok_dev, model_dim = y_next.shape
        seq_dev = owner.shape[1] // n_ep
        per_pair = seq_dev // n_ep
        owner_grid = owner[0].reshape(n_ep, seq_dev)
        src_dev = owner_grid // seq_dev
        positions = jnp.arange(seq_dev)
        send_rank = jnp.argsort(jnp.where(src_dev == dev_index, 0, seq_dev) + positions, axis=1)[:, :per_pair]
        send_seq = jnp.take_along_axis(owner_grid, send_rank, axis=1).reshape(seq_dev) - dev_index * seq_dev
        y_seqs = y_next.reshape(n_micro, seq_dev, tok_dev // seq_dev, model_dim)
        outgoing = jnp.take(y_seqs, send_seq, axis=1)
        incoming = lax.all_to_all(outgoing, 'ep', 1, 1, tiled=True)
        my_src = lax.dynamic_index_in_dim(src_dev, dev_index, 0, keepdims=False)
        arrival = jnp.argsort(my_src * seq_dev + positions)
        y_owned = jnp.take(incoming, jnp.argsort(arrival), axis=1)
        z_owned = attend_local(y_owned, norm_w[0], w_q[0], w_k[0], w_v[0], w_o[0])
        return z_owned.reshape(n_micro, tok_dev, model_dim)[None]

    tok_spec = P(group_axes, None, 'ep', None)
    weight_spec = P('pp', None, None)
    in_specs = (P(group_axes, None, 'ep', None, None), tok_spec, tok_spec, tok_spec, tok_spec, P(group_axes, None), P('pp', None), weight_spec, weight_spec, weight_spec, weight_spec)
    return jax.shard_map(device_step, mesh=mesh, in_specs=in_specs, out_specs=tok_spec, check_vma=False)
```

profile of v0, /device:TPU:0, one launch (start us, length us, event | category | flops | bytes accessed | tf_op | source)
XLA Modules:
  0.0 1052.6 jit_solution(16353507478932439346)
XLA Ops:
  0.0 39.6 %copy.88 = bf16[1,1,96,32,7168]{4,2,3,1,0:T(8,128)(2,1)} copy(bf16[1,1,96,32,7168]{4,3,2,1,0:T(8,128)(2,1)} %param.13) | data formatting | bytes 88080384 | tf_op args[0]
  39.6 0.0 copy-start.1
  39.6 0.0 copy-start.2
  39.6 0.0 copy-start.3
  39.6 11.9 %all-to-all-start = ((bf16[1,96,32,7168]{3,1,0,2:T(8,128)(2,1)}), bf16[1,96,32,7168]{3,1,0,2:T(8,128)(2,1)}, u32[]{:S(2)}, u32[]{:S(2)}) async-start(bf16[1,96,32,7168]{3,1,0,2:T(8,128)(2,1)} %bitcast.149), calls=%async_computation | async-start | bytes 88080384 | tf_op jit(solution)/shard_map/all_to_all | solution.py:55
  51.5 0.0 copy-done.1
  51.5 0.0 copy-done.2
  51.6 0.1 copy.57
  51.7 0.1 reshape.268
  51.8 0.0 copy-done.3
  51.9 0.1 copy.58
  52.0 475.4 %all-to-all-done = bf16[1,96,32,7168]{3,1,0,2:T(8,128)(2,1)} async-done(((bf16[1,96,32,7168]{3,1,0,2:T(8,128)(2,1)}), bf16[1,96,32,7168]{3,1,0,2:T(8,128)(2,1)}, u32[]{:S(2)}, u32[]{:S(2)}) %all-to-all-start) | async-done | bytes 44040224 | tf_op jit(solution)/shard_map/all_to_all | solution.py:55
  527.4 39.8 %copy.56 = bf16[1,96,4,8,7168]{4,3,1,2,0:T(8,128)(2,1)} copy(bf16[1,96,4,8,7168]{4,1,3,2,0:T(8,128)(2,1)} %bitcast.3) | data formatting | bytes 88080384 | tf_op jit(solution)/shard_map/all_to_all | solution.py:55
  567.2 97.6 %gather_fusion = bf16[2048,7168]{1,0:T(8,128)(2,1)} fusion(bf16[1,3072,7168]{2,1,0:T(8,128)(2,1)} %bitcast.148, s32[2048]{0:T(1024)S(1)} %reshape.268), kind=kCustom, calls=%fused_computation.2 | custom fusion | bytes 58736640 | tf_op jit(solution)/shard_map/vmap()/gather | solution.py:39
  664.8 23.2 %fusion.7 = f32[256,7168]{1,0:T(8,128)} fusion(bf16[2048,7168]{1,0:T(8,128)(2,1)} %gather_fusion, f32[256,8]{1,0:T(8,128)S(1)} %copy.58), kind=kLoop, calls=%fused_computation.12 | loop fusion | flops 42205184 | bytes 36708352 | tf_op jit(solution)/shard_map/reduce_sum | solution.py:41
  688.0 0.0 copy-start.6
  688.0 7.0 fusion.24
  695.0 2.5 collective-permute-start
  697.4 0.5 broadcast.261
  697.9 0.0 copy-done.6
  697.9 0.6 reduce.11
  698.5 0.1 reshape_squeeze.6
  698.6 0.1 copy.48
  698.7 0.6 sort.48
  699.4 0.1 copy.52
  699.5 0.1 reshape.274
  699.6 0.7 gather_fusion.1
  700.2 0.1 reshape.277
  700.3 0.1 copy.53
  700.4 0.1 copy.54
  700.5 0.1 sub.45
  700.6 76.0 %collective-permute-done = bf16[1,256,7168]{2,1,0:T(8,128)(2,1)} collective-permute-done((bf16[1,256,7168]{2,1,0:T(8,128)(2,1)}, bf16[1,256,7168]{2,1,0:T(8,128)(2,1)}, u32[]{:S(2)}, u32[]{:S(2)}) %collective-permute-start) | collective-permute-done | bytes 3670048 | tf_op jit(solution)/shard_map/ppermute | solution.py:57
  776.6 4.7 gather_fusion.2
  781.3 4.3 bitcast_select_fusion.1
  785.6 5.3 all-to-all-start.1
  790.8 0.0 copy-start.5
  790.9 0.2 multiply_reduce_fusion
  791.1 1.0 sort.49
  792.0 1.0 sort.50
  793.0 0.6 iota_compare_fusion
  793.6 39.5 %all-to-all-done.1 = bf16[1,8,32,7168]{3,2,0,1:T(8,128)(2,1)} async-done(((bf16[1,8,32,7168]{3,2,0,1:T(8,128)(2,1)}), bf16[1,8,32,7168]{3,2,0,1:T(8,128)(2,1)}, u32[]{:S(2)}, u32[]{:S(2)}) %all-to-all-start.1) | async-done | bytes 3670048 | tf_op jit(solution)/shard_map/all_to_all | solution.py:68
  833.1 4.7 gather_fusion.3
  837.7 3.1 fusion.21
  840.9 0.0 copy-done.5
  840.9 46.8 %fusion.52 = bf16[8,4,64,8,128]{4,3,2,1,0:T(8,128)(2,1)} fusion(bf16[1,7168,8192]{2,1,0:T(8,128)(2,1)} %param.22, f32[7168]{0:T(1024)S(1)} %bitcast.150, f32[8,32]{1,0:T(8,128)S(1)} %add_rsqrt_fusion, bf16[8,32,7168]{2,1,0:T(8,128)(2,1)} %gather_fusion.3, pred[8]{0:T(512)(128)(4,1)S(1)} %compare_and_fusion), kind=kOutput, calls=%fused_computation.53 | convolution fusion | flops 30076043264 | bytes 125334536 | tf_op jit(solution)/shard_map/msld,de->msle/dot_general | solution.py:18
  887.7 46.6 %fusion.46 = bf16[8,4,64,8,128]{4,3,2,1,0:T(8,128)(2,1)} fusion(bf16[1,7168,8192]{2,1,0:T(8,128)(2,1)} %param.21, f32[7168]{0:T(1024)S(1)} %bitcast.151, f32[8,32]{1,0:T(8,128)S(1)} %add_rsqrt_fusion, bf16[8,32,7168]{2,1,0:T(8,128)(2,1)} %gather_fusion.3, pred[8]{0:T(512)(128)(4,1)S(1)} %compare_and_fusion), kind=kOutput, calls=%fused_computation.51 | convolution fusion | flops 30076043264 | bytes 125334536 | tf_op jit(solution)/shard_map/msld,de->msle/dot_general | solution.py:18
  934.3 46.8 %fusion.49 = bf16[8,4,64,8,128]{4,3,2,1,0:T(8,128)(2,1)} fusion(bf16[1,7168,8192]{2,1,0:T(8,128)(2,1)} %param.20, f32[7168]{0:T(1024)S(1)} %bitcast.152, f32[8,32]{1,0:T(8,128)S(1)} %add_rsqrt_fusion, bf16[8,32,7168]{2,1,0:T(8,128)(2,1)} %gather_fusion.3, pred[8]{0:T(512)(128)(4,1)S(1)} %compare_and_fusion), kind=kOutput, calls=%fused_computation.52 | convolution fusion | flops 30076043264 | bytes 125334536 | tf_op jit(solution)/shard_map/msld,de->msle/dot_general | solution.py:18
  981.2 0.0 copy-start.4
  981.2 5.8 fusion.27
  986.9 0.0 copy-start
  986.9 3.2 copy-done
  990.1 0.0 copy-done.4
  990.1 3.0 fusion.74
  993.2 12.1 %fusion.85 = bf16[8,32,64,128]{3,1,2,0:T(8,128)(2,1)} fusion(bf16[8,4,64,8,128]{4,3,2,1,0:T(8,128)(2,1)} %fusion.52, f32[8,64,32]{2,1,0:T(8,128)S(1)} %fusion.74, f32[8,64,32,32]{2,3,1,0:T(8,128)} %copy-done, pred[32,32]{0,1:T(8,128)(4,1)S(1)} %copy-done.4), kind=kOutput, calls=%fused_computation.42.clone.1 | convolution fusion | flops 140001312 | bytes 10552320 | tf_op jit(solution)/shard_map/mshqk,mskhe->msqhe/dot_general | solution.py:27
  1005.3 47.1 %fusion.20 = bf16[1,8,32,7168]{3,2,1,0:T(8,128)(2,1)} fusion(bf16[64,128,7168,1]{2,1,0,3:T(8,128)(2,1)} %bitcast.28, bf16[8,32,7168]{2,1,0:T(8,128)(2,1)} %gather_fusion.3, pred[8]{0:T(512)(128)(4,1)S(1)} %compare_and_fusion, bf16[8,32,64,128]{3,1,2,0:T(8,128)(2,1)} %fusion.85), kind=kOutput, calls=%fused_computation.24 | convolution fusion | flops 30075781120 | bytes 128974856 | tf_op jit(solution)/shard_map/msqhe,hed->msqd/dot_general | solution.py:28
  (18 shorter events, 0.1 us)
Async XLA Ops:
  39.6 11.9 %copy-start.1 = (s32[1,1,256,8]{2,3,1,0:T(8,128)S(1)}, s32[1,1,256,8]{2,3,1,0:T(8,128)}, u32[]{:S(2)}) copy-start(s32[1,1,256,8]{2,3,1,0:T(8,128)} %param.15) | copy-start | bytes 24580
  39.6 11.9 %copy-start.2 = (s32[1,1,256,8]{2,3,1,0:T(8,128)S(1)}, s32[1,1,256,8]{2,3,1,0:T(8,128)}, u32[]{:S(2)}) copy-start(s32[1,1,256,8]{2,3,1,0:T(8,128)} %param.14) | copy-start | bytes 24580
  39.6 12.2 %copy-start.3 = (f32[1,1,256,8]{2,3,1,0:T(8,128)S(1)}, f32[1,1,256,8]{2,3,1,0:T(8,128)}, u32[]{:S(2)}) copy-start(f32[1,1,256,8]{2,3,1,0:T(8,128)} %param.16) | copy-start | bytes 24580
  39.6 487.7 %all-to-all-start = ((bf16[1,96,32,7168]{3,1,0,2:T(8,128)(2,1)}), bf16[1,96,32,7168]{3,1,0,2:T(8,128)(2,1)}, u32[]{:S(2)}, u32[]{:S(2)}) async-start(bf16[1,96,32,7168]{3,1,0,2:T(8,128)(2,1)} %bitcast.149), calls=%async_computation | async-start | bytes 88080384 | tf_op jit(solution)/shard_map/all_to_all | solution.py:55
  688.0 9.9 copy-start.6
  695.0 81.6 %collective-permute-start = (bf16[1,256,7168]{2,1,0:T(8,128)(2,1)}, bf16[1,256,7168]{2,1,0:T(8,128)(2,1)}, u32[]{:S(2)}, u32[]{:S(2)}) collective-permute-start(bf16[1,256,7168]{2,1,0:T(8,128)(2,1)} %fusion.24), channel_id=1, source_target_pairs={{0,4},{4,0},{1,5},{5,1},{2,6},{6,2},{3,7},{7,3}} | collective-permute-start | bytes 11010056 | tf_op jit(solution)/shard_map/ppermute | solution.py:57
  785.6 47.5 %all-to-all-start.1 = ((bf16[1,8,32,7168]{3,2,0,1:T(8,128)(2,1)}), bf16[1,8,32,7168]{3,2,0,1:T(8,128)(2,1)}, u32[]{:S(2)}, u32[]{:S(2)}) async-start(bf16[1,8,32,7168]{3,2,0,1:T(8,128)(2,1)} %bitcast_select_fusion.1), calls=%async_computation.1 | async-start | bytes 7340032 | tf_op jit(solution)/shard_map/all_to_all | solution.py:68
  790.8 50.1 %copy-start.5 = (f32[1,7168]{1,0:T(1,128)S(1)}, f32[1,7168]{1,0:T(1,128)}, u32[]{:S(2)}) copy-start(f32[1,7168]{1,0:T(1,128)} %param.19) | copy-start | bytes 86020
  981.2 9.0 copy-start.4
  986.9 3.2 copy-start
where the time goes:
time: 1060 us; the launch traced here: 1050 us
  waiting for transfers between devices  591 us (56%)
  matrix products  205 us (19%)
  local copies, waits for them, and re-layouts  192 us (18%)
  other arithmetic  44.7 us (4%)
  starting transfers between devices  19.6 us (2%)
    all_to_all x1, waiting for transfers between devices, device_step(): recv_out = lax.all_to_all(out_local, 'ep', 2, 1, tiled=True)  475 us
    dot_general x3, matrix products, project(): jnp.einsum('msld,de->msle', normed, weight, preferred_element_type=jnp.fl...  140 us
    gather x4, local copies, waits for them, and re-layouts, combine_home(): out_table[row_ids]  97.8 us
    ppermute x1, waiting for transfers between devices, device_step(): y_next = lax.ppermute(y_home, 'pp', next_rank)  76 us
    dot_general x1, matrix products, attend_local(): jnp.einsum('msqhe,hed->msqd', head_mix, w_o.reshape(n_heads, HEAD_DIM, mo...  47.1 us
    unnamed x16, local copies, waits for them, and re-layouts  43.4 us
    all_to_all x1, local copies, waits for them, and re-layouts, device_step(): recv_out = lax.all_to_all(out_local, 'ep', 2, 1, tiled=True)  39.8 us
    all_to_all x1, waiting for transfers between devices, device_step(): incoming = lax.all_to_all(outgoing, 'ep', 1, 1, tiled=True)  39.5 us
  transfers between devices with their start and end apart: 3, of which 3 were waited for; matrix products, arithmetic and copies ran while one was open for 1% of the time, Pallas kernels for 0%

commit v1 on v0

v1 whole, which is shorter than its diff:
```python
import functools

import jax
import jax.numpy as jnp
from jax import lax
from jax.experimental import pallas as pl
from jax.experimental.pallas import tpu as pltpu
from jax.sharding import PartitionSpec as P

HEAD_DIM = 128
NORM_EPS = 1e-6
F32, BF16 = jnp.float32, jnp.bfloat16
MESH = pl.DeviceIdType.MESH
VMEM_LIMIT = 66_000_000


def combine_kernel(n_ep, n_stages, dk, nk, o_hbm, info_ref, h_hbm, y_hbm, obuf, hbuf, w3, perm, send_a, recv_a, keep, send_b, recv_b,
                   send_c, o_sem, h_sem, sa_sem, ra_sem, sb_sem, rb_sem, sc_sem, rc_sem):
    me = lax.axis_index('ep')
    rank = lax.axis_index('pp')
    core_peer = me + 1 - 2 * lax.rem(me, 2)
    x_peer = lax.rem(me + 2, n_ep)
    next_rank = lax.rem(rank + 1, n_stages)
    prev_rank = lax.rem(rank + n_stages - 1, n_stages)
    n_exp, cap_dev, n_slot = obuf.shape[1], obuf.shape[2], w3.shape[-1]
    n_tok = h_hbm.shape[0]
    n_dest = n_tok // n_ep

    def o_copy(k, o):
        j = lax.rem(me + o, n_ep)
        return pltpu.make_async_copy(o_hbm.at[:, pl.ds(pl.multiple_of(j * cap_dev, cap_dev), cap_dev), pl.ds(pl.multiple_of(k * dk, dk), dk)],
                                     obuf.at[o], o_sem.at[o])

    def h_copy(k):
        return pltpu.make_async_copy(h_hbm.at[:, pl.ds(pl.multiple_of(k * dk, dk), dk)], hbuf, h_sem.at[0])

    def a_copy(k):
        return pltpu.make_async_remote_copy(send_a.at[lax.rem(k, 2)], recv_a.at[k], sa_sem.at[lax.rem(k, 2)], ra_sem.at[k],
                                            device_id={'ep': core_peer}, device_id_type=MESH)

    def b_copy(k):
        return pltpu.make_async_remote_copy(send_b.at[lax.rem(k, 4)], recv_b.at[k], sb_sem.at[lax.rem(k, 4)], rb_sem.at[k],
                                            device_id={'ep': x_peer}, device_id_type=MESH)

    def c_copy(k):
        return pltpu.make_async_remote_copy(send_c.at[lax.rem(k, 2)], y_hbm.at[:, pl.ds(pl.multiple_of(k * dk, dk), dk)], sc_sem.at[lax.rem(k, 2)],
                                            rc_sem.at[k], device_id={'pp': next_rank}, device_id_type=MESH)

    for o in range(n_ep):
        o_copy(0, o).start()
    h_copy(0).start()

    barrier = pltpu.get_barrier_semaphore()
    pl.semaphore_signal(barrier, inc=1, device_id={'ep': core_peer}, device_id_type=MESH)
    pl.semaphore_signal(barrier, inc=1, device_id={'ep': x_peer}, device_id_type=MESH)
    pl.semaphore_signal(barrier, inc=1, device_id={'pp': prev_rank}, device_id_type=MESH)

    rb = 32

    def build(step, _):
        o = step // (n_tok // rb)
        row = pl.multiple_of(lax.rem(step, n_tok // rb) * rb, rb)
        rows = info_ref[lax.rem(me + o, n_ep), pl.ds(row, rb), :]
        slot = lax.broadcasted_iota(jnp.int32, (rb, n_slot), 1).astype(F32)
        w = jnp.zeros((rb, n_slot), F32)
        for c in range(8):
            w = jnp.where(rows[:, c:c + 1] == slot, rows[:, 8 + c:9 + c], w)
        high = w.astype(BF16)
        rest = w - high.astype(F32)
        mid = rest.astype(BF16)
        w3[o, 0, pl.ds(row, rb), :] = high
        w3[o, 1, pl.ds(row, rb), :] = mid
        w3[o, 2, pl.ds(row, rb), :] = (rest - mid.astype(F32)).astype(BF16)
        return 0

    lax.fori_loop(0, n_ep * (n_tok // rb), build, 0)
    home = info_ref[me, :, 16:17]
    perm[...] = (home == lax.broadcasted_iota(jnp.int32, (n_tok, n_tok), 1).astype(F32)).astype(F32).astype(BF16)
    pl.semaphore_wait(barrier, 3)

    def partial_sums(k):
        @pl.when(k >= 2)
        def _():
            a_copy(k - 2).wait_send()

        @pl.when(k >= 4)
        def _():
            b_copy(k - 4).wait_send()

        for o in range(n_ep):
            o_copy(k, o).wait()
            rows = obuf[o].reshape(n_exp * cap_dev, dk)
            part = jnp.dot(w3[o, 0], rows, preferred_element_type=F32)
            part += jnp.dot(w3[o, 1], rows, preferred_element_type=F32)
            part += jnp.dot(w3[o, 2], rows, preferred_element_type=F32)
            if o == 0:
                h_copy(k).wait()
                part += jnp.dot(perm[...], hbuf[...], preferred_element_type=F32)
            place = pl.ds(pl.multiple_of(lax.rem(me + o, n_ep) * n_dest, n_dest), n_dest)
            keep[lax.rem(k, 4), place, :] = part[0:n_dest]
            send_b[lax.rem(k, 4), place, :] = part[n_dest:2 * n_dest]
            send_a[lax.rem(k, 2), 0, place, :] = part[2 * n_dest:3 * n_dest]
            send_a[lax.rem(k, 2), 1, place, :] = part[3 * n_dest:4 * n_dest]

            @pl.when(k + 1 < nk)
            def _():
                o_copy(k + 1, o).start()
                if o == 0:
                    h_copy(k + 1).start()

        a_copy(k).start()

    def across_x(k):
        a_copy(k).wait_recv()
        keep[lax.rem(k, 4)] = keep[lax.rem(k, 4)] + recv_a[k, 0]
        send_b[lax.rem(k, 4)] = send_b[lax.rem(k, 4)] + recv_a[k, 1]
        b_copy(k).start()

    def across_y(k):
        b_copy(k).wait_recv()

        @pl.when(k >= 2)
        def _():
            c_copy(k - 2).wait_send()

        send_c[lax.rem(k, 2)] = (keep[lax.rem(k, 4)] + recv_b[k]).astype(BF16)
        c_copy(k).start()

    def step(k, _):
        @pl.when(k < nk)
        def _():
            partial_sums(k)

        @pl.when((k >= 1) & (k < nk + 1))
        def _():
            across_x(k - 1)

        @pl.when(k >= 3)
        def _():
            across_y(k - 3)

        return 0

    lax.fori_loop(0, nk + 3, step, 0)

    for k in range(nk - 2, nk):
        a_copy(k).wait_send()
        c_copy(k).wait_send()
    for k in range(nk - 4, nk):
        b_copy(k).wait_send()

    def arrive(k, _):
        c_copy(k).wait_recv()
        return 0

    lax.fori_loop(0, nk, arrive, 0)


def combine_and_send(out_local, info, resid, n_ep, n_stages, dk=512):
    n_exp, capacity, dim = out_local.shape
    n_tok = resid.shape[0]
    cap_dev = capacity // n_ep
    n_slot = n_exp * cap_dev
    nk = dim // dk
    any_spec = pl.BlockSpec(memory_space=pl.ANY)
    dma = pltpu.SemaphoreType.DMA
    return pl.pallas_call(
        functools.partial(combine_kernel, n_ep, n_stages, dk, nk),
        out_shape=jax.ShapeDtypeStruct((n_tok, dim), BF16),
        in_specs=[any_spec, pl.BlockSpec(memory_space=pltpu.VMEM), any_spec],
        out_specs=any_spec,
        scratch_shapes=[
            pltpu.VMEM((n_ep, n_exp, cap_dev, dk), BF16),
            pltpu.VMEM((n_tok, dk), BF16),
            pltpu.VMEM((n_ep, 3, n_tok, n_slot), BF16),
            pltpu.VMEM((n_tok, n_tok), BF16),
            pltpu.VMEM((2, 2, n_tok, dk), F32),
            pltpu.VMEM((nk, 2, n_tok, dk), F32),
            pltpu.VMEM((4, n_tok, dk), F32),
            pltpu.VMEM((4, n_tok, dk), F32),
            pltpu.VMEM((nk, n_tok, dk), F32),
            pltpu.VMEM((2, n_tok, dk), BF16),
            dma((n_ep,)), dma((1,)), dma((2,)), dma((nk,)), dma((4,)), dma((nk,)), dma((2,)), dma((nk,)),
        ],
        compiler_params=pltpu.CompilerParams(collective_id=0, has_side_effects=True, vmem_limit_bytes=VMEM_LIMIT),
        name='combine_and_send',
    )(out_local, info, resid)


def attend_heads(q, k, v, seq_len, blk=128):
    n_tok, width = q.shape
    row = lax.broadcasted_iota(jnp.int32, (blk, blk), 0)
    col = lax.broadcasted_iota(jnp.int32, (blk, blk), 1)
    seen = (row >= col) & (row // seq_len == col // seq_len)
    heads = []
    for h in range(width // HEAD_DIM):
        tiles = []
        for t in range(n_tok // blk):
            at = (slice(t * blk, (t + 1) * blk), slice(h * HEAD_DIM, (h + 1) * HEAD_DIM))
            s = lax.dot_general(q[at], k[at], (((1,), (1,)), ((), ())), preferred_element_type=F32) * (HEAD_DIM ** -0.5)
            s = jnp.where(seen, s, -1e30)
            e = jnp.exp(s - jnp.max(s, axis=1, keepdims=True))
            p = (e / jnp.sum(e, axis=1, keepdims=True)).astype(BF16)
            tiles.append(jnp.dot(p, v[at], preferred_element_type=F32).astype(BF16))
        heads.append(jnp.concatenate(tiles, axis=0))
    return jnp.concatenate(heads, axis=1)


def qkv_kernel(n_blk, seq_len, y_ref, nw_ref, wq_ref, wk_ref, wv_ref, a_ref, x_scr, q_scr, k_scr, v_scr):
    i = pl.program_id(0)
    n_tok = y_ref.shape[0]
    rb = 16

    @pl.when(i == 0)
    def _():
        def norm(step, _):
            rows = pl.ds(pl.multiple_of(step * rb, rb), rb)
            y = y_ref[rows, :].astype(F32)
            inv = lax.rsqrt(jnp.mean(y * y, axis=1, keepdims=True) + NORM_EPS)
            x_scr[rows, :] = (y * inv * nw_ref[...]).astype(BF16)
            return 0

        lax.fori_loop(0, n_tok // rb, norm, 0)

    def attend():
        a_ref[...] = attend_heads(q_scr[...], k_scr[...], v_scr[...], seq_len)

    def project():
        q = jnp.dot(x_scr[...], wq_ref[...], preferred_element_type=F32).astype(BF16)
        k = jnp.dot(x_scr[...], wk_ref[...], preferred_element_type=F32).astype(BF16)
        v = jnp.dot(x_scr[...], wv_ref[...], preferred_element_type=F32).astype(BF16)
        q_scr[...] = q
        k_scr[...] = k
        v_scr[...] = v

    @pl.when(i == 0)
    def _():
        project()

    @pl.when((i > 0) & (i < n_blk))
    def _():
        attend()
        project()

    @pl.when(i == n_blk)
    def _():
        attend()


def qkv_attend(y, norm_w, w_q, w_k, w_v, seq_len, bn=256):
    n_tok, dim = y.shape
    width = w_q.shape[1]
    n_blk = width // bn
    w_spec = pl.BlockSpec((dim, bn), lambda i: (0, jnp.minimum(i, n_blk - 1)))
    return pl.pallas_call(
        functools.partial(qkv_kernel, n_blk, seq_len),
        grid=(n_blk + 1,),
        out_shape=jax.ShapeDtypeStruct((n_tok, width), BF16),
        in_specs=[pl.BlockSpec((n_tok, dim), lambda i: (0, 0), pipeline_mode=pl.Buffered(1)),
                  pl.BlockSpec((1, dim), lambda i: (0, 0), pipeline_mode=pl.Buffered(1)), w_spec, w_spec, w_spec],
        out_specs=pl.BlockSpec((n_tok, bn), lambda i: (0, jnp.maximum(i - 1, 0))),
        scratch_shapes=[pltpu.VMEM((n_tok, dim), BF16)] + [pltpu.VMEM((n_tok, bn), BF16)] * 3,
        compiler_params=pltpu.CompilerParams(dimension_semantics=('arbitrary',), vmem_limit_bytes=VMEM_LIMIT),
        name='qkv_attend',
    )(y, norm_w, w_q, w_k, w_v)


def out_kernel(seq_len, pos_ref, a_ref, y_ref, wo_ref, z_ref):
    proj = jnp.dot(a_ref[...], wo_ref[...], preferred_element_type=F32).astype(BF16)
    z = (y_ref[...].astype(F32) + proj.astype(F32)).astype(BF16)
    for s in range(z.shape[0] // seq_len):
        z_ref[pl.ds(pl.multiple_of(pos_ref[s] * seq_len, seq_len), seq_len), :] = z[s * seq_len:(s + 1) * seq_len]


def out_project(pos, a, y, w_o, seq_len, bn=256):
    n_tok, width = a.shape
    dim = w_o.shape[1]
    return pl.pallas_call(
        functools.partial(out_kernel, seq_len),
        grid_spec=pltpu.PrefetchScalarGridSpec(
            num_scalar_prefetch=1,
            grid=(dim // bn,),
            in_specs=[pl.BlockSpec((n_tok, width), lambda i, pos: (0, 0), pipeline_mode=pl.Buffered(1)),
                      pl.BlockSpec((n_tok, bn), lambda i, pos: (0, i)), pl.BlockSpec((width, bn), lambda i, pos: (0, i))],
            out_specs=pl.BlockSpec((n_tok, bn), lambda i, pos: (0, i)),
        ),
        out_shape=jax.ShapeDtypeStruct((n_tok, dim), BF16),
        compiler_params=pltpu.CompilerParams(dimension_semantics=('arbitrary',), vmem_limit_bytes=VMEM_LIMIT),
        name='out_project',
    )(pos, a, y, w_o)


def arrival_order(owner_row, n_ep):
    seq_dev = owner_row.shape[0] // n_ep
    grid = owner_row.reshape(n_ep, seq_dev)
    key = (grid // seq_dev) * seq_dev + jnp.arange(seq_dev)
    place = jnp.sum(key[:, None, :] < key[:, :, None], axis=2)
    chosen = (place[:, None, :] == jnp.arange(seq_dev)[:, None]).astype(jnp.int32)
    return jnp.sum(chosen * grid[:, None, :], axis=2), jnp.sum(chosen * jnp.arange(seq_dev), axis=2)


def solution(mesh):
    n_stages = mesh.shape['pp']
    n_ep = mesh.shape['ep']
    group_axes = ('data', 'pp')

    def device_step(expert_out, expert_id, slot_id, gate, resid, owner, norm_w, w_q, w_k, w_v, w_o):
        me = lax.axis_index('ep')
        out_local, h = expert_out[0, 0], resid[0, 0]
        n_exp, capacity, dim = out_local.shape
        cap_dev = capacity // n_ep
        n_tok = h.shape[0]
        n_seq = owner.shape[1]
        seq_dev = n_seq // n_ep
        seq_len = n_tok // seq_dev
        n_slot = n_exp * cap_dev

        owner_next = lax.ppermute(owner[0], 'pp', [((r + 1) % n_stages, r) for r in range(n_stages)])
        ids, slots = expert_id[0, 0], slot_id[0, 0]
        index = jnp.where(slots >= 0, ids * cap_dev + slots - me * cap_dev, -1).astype(F32)
        local = jnp.broadcast_to(jnp.arange(n_tok, dtype=F32)[:, None], (n_tok, 1))
        table = lax.all_gather(jnp.concatenate([index, gate[0, 0], local], axis=1), 'ep', axis=0, tiled=True)
        dest_seqs, _ = arrival_order(owner_next, n_ep)
        relative = jnp.bitwise_xor(me, jnp.array([0, 2, 1, 3]))
        pick = dest_seqs[relative].reshape(n_ep, n_ep, seq_dev // n_ep).transpose(1, 0, 2).reshape(n_seq)
        info = table.reshape(n_seq, seq_len * 17)[pick].reshape(n_ep, n_tok, 17)
        info = jnp.concatenate([info[:, :, :8] - (me * n_slot).astype(F32), info[:, :, 8:]], axis=2)

        y = combine_and_send(out_local, info, h, n_ep, n_stages)

        _, rows = arrival_order(owner[0], n_ep)
        pos = lax.dynamic_index_in_dim(rows, me, 0, keepdims=False).astype(jnp.int32)
        heads = qkv_attend(y, norm_w, w_q[0], w_k[0], w_v[0], seq_len)
        return out_project(pos, heads, y, w_o[0], seq_len)[None, None]

    tok_spec = P(group_axes, None, 'ep', None)
    weight_spec = P('pp', None, None)
    in_specs = (P(group_axes, None, 'ep', None, None), tok_spec, tok_spec, tok_spec, tok_spec, P(group_axes, None), P('pp', None), weight_spec,
                weight_spec, weight_spec, weight_spec)
    return jax.shard_map(device_step, mesh=mesh, in_specs=in_specs, out_specs=tok_spec, check_vma=False)
```

time: 1060 us -> 404 us (0.38)
  waiting for transfers between devices: 591 us -> 0.01 us
  Pallas kernels: 0 us -> 383 us
  matrix products: 205 us -> 0 us
  local copies, waits for them, and re-layouts: 192 us -> 4 us
  other arithmetic: 44.7 us -> 5.22 us
  starting transfers between devices: 19.6 us -> 3.37 us
    all_to_all x2 -> x0, waiting for transfers between devices: 515 us -> none  [the longest x1 475 us: device_step(): recv_out = lax.all_to_all(out_local, 'ep', 2, 1, tiled=True)]
    pallas_call x0 -> x3, Pallas kernels: none -> 383 us  [the longest x1 178 us: combine_and_send(): pl.pallas_call(functools.partial(combine_kernel, n_ep, n_stages, dk, nk),...]
    dot_general x6 -> x0, matrix products: 205 us -> none  [the longest x3 140 us: project(): jnp.einsum('msld,de->msle', normed, weight, preferred_element_type=jnp.fl...]
    gather x11 -> x3, local copies, waits for them, and re-layouts: 108 us -> 1.27 us  [the longest x2 0.65 us: device_step(): dest_seqs[relative].reshape(n_ep, n_ep, seq_dev // n_ep).transpose(1, 0, 2)]
    ppermute x1, waiting for transfers between devices: 76 us -> 0.01 us  [device_step(): lax.ppermute(owner[0], 'pp', [((r + 1) % n_stages, r) for r in range(n_st...]
    unnamed x16 -> x1, local copies, waits for them, and re-layouts: 43.4 us -> 0.51 us
    all_to_all x1 -> x0, local copies, waits for them, and re-layouts: 39.8 us -> none  [device_step(): recv_out = lax.all_to_all(out_local, 'ep', 2, 1, tiled=True)]
    reduce_sum x2 -> x4, other arithmetic: 26.4 us -> 0.74 us  [the longest x2 0.43 us: arrival_order(): place = jnp.sum(key[:, None, :] < key[:, :, None], axis=2)]
  transfers between devices with their start and end apart: 3 -> 1, of which waited for: 3 -> 0; matrix products, arithmetic and copies ran while one was open for 1% -> 1% of each run, Pallas kernels for 0% -> 0%
where the time goes in v1:
time: 404 us
  Pallas kernels  383 us (95%)
  blocking collectives  8.29 us (2%)
  other arithmetic  5.22 us (1%)
    pallas_call x1, Pallas kernels, combine_and_send(): pl.pallas_call(functools.partial(combine_kernel, n_ep, n_stages, dk, nk),...  178 us
    pallas_call x1, Pallas kernels, qkv_attend(): pl.pallas_call(functools.partial(qkv_kernel, n_blk, seq_len), grid=(n_blk...  149 us
    pallas_call x1, Pallas kernels, out_project(): pl.pallas_call(functools.partial(out_kernel, seq_len), grid_spec=pltpu.Pr...  55.6 us
    all_gather x1, blocking collectives, device_step(): lax.all_gather(jnp.concatenate([index, gate[0, 0], local], axis=1), 'ep',...  8.29 us
  transfers between devices with their start and end apart: 1, of which 0 were waited for; matrix products, arithmetic and copies ran while one was open for 1% of the time, Pallas kernels for 0%

profile of v1, /device:TPU:0, one launch (start us, length us, event | category | flops | bytes accessed | tf_op | source)
XLA Modules:
  0.0 403.5 jit_solution(3694993081635478220)
XLA Ops:
  0.0 3.4 collective-permute-start
  3.4 0.5 broadcast.192
  3.9 1.3 reduce.3
  5.2 0.7 compare_select_fusion.1
  5.9 0.1 reshape_squeeze.3
  6.0 0.2 convert_reduce_fusion.1
  6.2 0.2 select_reduce_fusion.1
  6.3 0.7 convert_bitcast_fusion
  7.1 0.7 pad_maximum_fusion.1
  7.8 8.3 %all_gather.3 = f32[1024,17]{0,1:T(8,128)S(1)} all-gather(f32[256,17]{0,1:T(8,128)S(1)} %pad_maximum_fusion.1), channel_id=1, replica_groups=mesh['data'=1,'pp'=2,'ep'=4] {'ep'}, dimensions={0}, use_global_device_ids=true | all-gather | bytes 87040 | tf_op jit(solution)/shard_map/all_gather | solution.py:322
  16.1 0.6 dynamic-slice_bitcast_fusion.pos_ref
  16.6 0.2 copy.25
  16.9 0.3 reshape.195
  17.1 0.0 collective-permute-done
  17.1 0.1 reshape.196
  17.2 0.2 convert_reduce_fusion
  17.5 0.2 select_reduce_fusion
  17.6 0.6 gather_fusion
  18.2 0.1 copy.26
  18.3 0.1 copy.27
  18.4 0.1 reshape.198
  18.5 0.6 gather_fusion.1
  19.1 0.6 reshape.199
  19.7 0.2 slice.13
  20.0 1.0 pad_maximum_fusion.info_ref
  21.0 177.6 %combine_and_send.1.y_ref = bf16[256,7168]{1,0:T(8,128)(2,1)} custom-call(bf16[96,32,7168]{2,1,0:T(8,128)(2,1)} %bitcast.18, f32[4,256,17]{2,1,0:T(8,128)} %pad_maximum_fusion.info_ref, bf16[256,7168]{1,0:T(8,128)(2,1)} %bitcast.19), custom_call_target="tpu_custom_call" | custom-call | tf_op jit(solution)/shard_map/combine_and_send/pallas_call | solution.py:167
  198.5 149.4 %qkv_attend.1.a_ref = bf16[256,8192]{1,0:T(8,128)(2,1)} custom-call(bf16[256,7168]{1,0:T(8,128)(2,1)} %combine_and_send.1.y_ref, f32[1,7168]{1,0:T(1,128)} %nw_ref.1, bf16[7168,8192]{1,0:T(8,128)(2,1)} %bitcast.9.wq_ref, bf16[7168,8192]{1,0:T(8,128)(2,1)} %bitcast.10.wk_ref, bf16[7168,8192]{1,0:T(8,128)(2,1)} %bitcast.11.wv_ref), custom_call_target="tpu_custom_call" | custom-call | tf_op jit(solution)/shard_map/qkv_attend/pallas_call | solution.py:255
  347.9 55.6 %out_project.1 = bf16[256,7168]{1,0:T(8,128)(2,1)} custom-call(s32[8]{0:T(128)} %dynamic-slice_bitcast_fusion.pos_ref, bf16[256,8192]{1,0:T(8,128)(2,1)} %qkv_attend.1.a_ref, bf16[256,7168]{1,0:T(8,128)(2,1)} %combine_and_send.1.y_ref, bf16[8192,7168]{1,0:T(8,128)(2,1)} %bitcast.12.wo_ref), custom_call_target="tpu_custom_call" | custom-call | tf_op jit(solution)/shard_map/out_project/pallas_call | solution.py:278
  (7 shorter events, 0.1 us)
Async XLA Ops:
  0.0 17.1 %collective-permute-start = (s32[32]{0:T(128)}, s32[32]{0:T(128)S(1)}, u32[]{:S(2)}, u32[]{:S(2)}) collective-permute-start(s32[32]{0:T(128)} %bitcast.22), channel_id=1, source_target_pairs={{4,0},{0,4},{5,1},{1,5},{6,2},{2,6},{7,3},{3,7}} | collective-permute-start | bytes 392 | tf_op jit(solution)/shard_map/ppermute | solution.py:318

commit v2 on v0

v2 whole, which is shorter than its diff:
```python
import functools

import jax
import jax.numpy as jnp
from jax import lax
from jax.experimental import pallas as pl
from jax.experimental.pallas import tpu as pltpu
from jax.sharding import PartitionSpec as P

HEAD_DIM = 128
NORM_EPS = 1e-6
F32, BF16 = jnp.float32, jnp.bfloat16
MESH = pl.DeviceIdType.MESH
VMEM_LIMIT = 66_000_000


def stage_kernel(n_ep, n_stages, dk, bn, seq_len, o_hbm, info_ref, h_hbm, nw_ref, wq_hbm, wk_hbm, wv_hbm, wo_hbm, z_hbm, obuf, hbuf, w3, perm,
                 send_a, recv_a, keep, send_b, recv_b, send_c, y_own, xbuf, wbuf, abuf, q_scr, k_scr, v_scr, zscr, recv_z, zout,
                 o_sem, h_sem, sa_sem, ra_sem, sb_sem, rb_sem, sc_sem, rc_sem, sx_sem, rx_sem, w_sem, sz_sem, rz_sem, out_sem,
                 a_free, b_free, z_free):
    me = lax.axis_index('ep')
    rank = lax.axis_index('pp')
    core = lax.rem(me, 2)
    core_peer = me + 1 - 2 * core
    x_peer = lax.rem(me + 2, n_ep)
    next_rank = lax.rem(rank + 1, n_stages)
    prev_rank = lax.rem(rank + n_stages - 1, n_stages)
    n_exp, cap_dev, n_slot = obuf.shape[1], obuf.shape[2], perm.shape[1] * 3
    n_tok, dim = h_hbm.shape
    n_slot = n_exp * cap_dev
    rows_g = n_tok // 2
    sub = rows_g // n_ep
    nk = dim // dk
    n_unit = 2 * nk
    ring_a, ring_b, ring_c = recv_a.shape[0], keep.shape[0], send_c.shape[0]
    width = abuf.shape[1]
    n_hp = width // bn
    n_ot = dim // bn
    n_w, ring_z, ring_r = wbuf.shape[0], zscr.shape[0], recv_z.shape[0]
    n_tile = 3 * n_hp + n_ot

    def col(k, w):
        return pl.ds(pl.multiple_of(k * w, w), w)

    def o_copy(u, o):
        j = lax.rem(me + o, n_ep)
        return pltpu.make_async_copy(o_hbm.at[:, col(j, cap_dev), col(lax.rem(u, nk), dk)], obuf.at[o], o_sem.at[o])

    def h_copy(u):
        return pltpu.make_async_copy(h_hbm.at[:, col(lax.rem(u, nk), dk)], hbuf, h_sem.at[0])

    def to_core(src, dst, s_sem, r_sem):
        return pltpu.make_async_remote_copy(src, dst, s_sem, r_sem, device_id={'ep': core_peer}, device_id_type=MESH)

    def a_copy(u):
        return to_core(send_a.at[lax.rem(u, 2)], recv_a.at[lax.rem(u, ring_a)], sa_sem.at[lax.rem(u, 2)], ra_sem.at[lax.rem(u, ring_a)])

    def b_copy(u):
        i = lax.rem(u, ring_b)
        return pltpu.make_async_remote_copy(send_b.at[i], recv_b.at[i], sb_sem.at[i], rb_sem.at[i], device_id={'ep': x_peer}, device_id_type=MESH)

    def c_copy(u):
        i = lax.rem(u, ring_c)
        return pltpu.make_async_remote_copy(send_c.at[i], y_own.at[u // nk, :, col(lax.rem(u, nk), dk)], sc_sem.at[i], rc_sem.at[u],
                                            device_id={'pp': next_rank}, device_id_type=MESH)

    def x_copy(g, p):
        at = xbuf.at[g, pl.ds(pl.multiple_of(core * rows_g + p * 32, 32), 32)]
        return to_core(at, at, sx_sem.at[p], rx_sem.at[g * (rows_g // 32) + p])

    def z_copy(t):
        theirs = pl.ds(pl.multiple_of((1 - core) * rows_g, rows_g), rows_g)
        return to_core(zscr.at[lax.rem(t, ring_z), theirs], recv_z.at[lax.rem(t, ring_r)], sz_sem.at[lax.rem(t, ring_z)], rz_sem.at[lax.rem(t, ring_r)])

    def out_copy(t):
        i = lax.rem(t, ring_z)
        return pltpu.make_async_copy(zout.at[i], z_hbm.at[col(t // n_ot, rows_g), col(lax.rem(t, n_ot), bn)], out_sem.at[i])

    def w_slot(s):
        return wbuf.at[lax.rem(s, n_w)], w_sem.at[lax.rem(s, n_w)]

    def qkv_tile(s, hp, kind):
        slot, sem = w_slot(s)
        return pltpu.make_async_copy((wq_hbm, wk_hbm, wv_hbm)[kind].at[:, col(core * n_hp + hp, bn)], slot, sem)

    def out_tile(s, t):
        slot, sem = w_slot(s)
        return pltpu.make_async_copy(wo_hbm.at[col(core, width), col(t, bn)], slot.at[pl.ds(0, width)], sem)

    def start_tile(s):
        at = lax.rem(s, n_tile)

        @pl.when(s < 2 * n_tile)
        def _():
            for kind in range(3):
                @pl.when((at < 3 * n_hp) & (lax.rem(at, 3) == kind))
                def _():
                    qkv_tile(s, at // 3, kind).start()

            @pl.when(at >= 3 * n_hp)
            def _():
                out_tile(s, at - 3 * n_hp).start()

    for o in range(n_ep):
        o_copy(0, o).start()
    h_copy(0).start()
    for s in range(n_w):
        qkv_tile(s, s // 3, s % 3).start()

    barrier = pltpu.get_barrier_semaphore()
    pl.semaphore_signal(barrier, inc=1, device_id={'ep': core_peer}, device_id_type=MESH)
    pl.semaphore_signal(barrier, inc=1, device_id={'ep': x_peer}, device_id_type=MESH)
    pl.semaphore_signal(barrier, inc=1, device_id={'pp': prev_rank}, device_id_type=MESH)

    def build(g):
        def block(step, _):
            o = step // n_ep
            part = lax.rem(step, n_ep) * sub
            rows = info_ref[lax.rem(me + o, n_ep), pl.ds(pl.multiple_of(g * rows_g + part, sub), sub), :]
            slot = lax.broadcasted_iota(jnp.int32, (sub, n_slot), 1).astype(F32)
            w = jnp.zeros((sub, n_slot), F32)
            for c in range(8):
                w = jnp.where(rows[:, c:c + 1] == slot, rows[:, 8 + c:9 + c], w)
            for t in range(3):
                high = w.astype(BF16)
                w3[o, pl.ds(pl.multiple_of(t * rows_g + part, sub), sub), :] = high
                w = w - high.astype(F32)
            return 0

        lax.fori_loop(0, n_ep * n_ep, block, 0)
        home = info_ref[me, pl.ds(pl.multiple_of(g * rows_g, rows_g), rows_g), 16:17]
        perm[...] = (home == lax.broadcasted_iota(jnp.int32, (rows_g, n_tok), 1).astype(F32)).astype(F32).astype(BF16)

    def partial_sums(u):
        @pl.when(lax.rem(u, nk) == 0)
        def _():
            build(u // nk)

        @pl.when(u >= 2)
        def _():
            a_copy(u - 2).wait_send()

        @pl.when(u >= ring_b)
        def _():
            b_copy(u - ring_b).wait_send()

        for o in range(n_ep):
            o_copy(u, o).wait()
            rows = obuf[o].reshape(n_slot, dk)
            split = jnp.dot(w3[o], rows, preferred_element_type=F32)
            part = split[:rows_g] + split[rows_g:2 * rows_g] + split[2 * rows_g:]
            if o == 0:
                h_copy(u).wait()
                part += jnp.dot(perm[...], hbuf[...], preferred_element_type=F32)
            place = pl.ds(pl.multiple_of(lax.rem(me + o, n_ep) * sub, sub), sub)
            keep[lax.rem(u, ring_b), place, :] = part[0:sub]
            send_b[lax.rem(u, ring_b), place, :] = part[sub:2 * sub]
            send_a[lax.rem(u, 2), 0, place, :] = part[2 * sub:3 * sub]
            send_a[lax.rem(u, 2), 1, place, :] = part[3 * sub:4 * sub]

            @pl.when(u + 1 < n_unit)
            def _():
                o_copy(u + 1, o).start()
                if o == 0:
                    h_copy(u + 1).start()

        @pl.when(u >= ring_a)
        def _():
            pl.semaphore_wait(a_free, 1)

        a_copy(u).start()

    def across_x(u):
        i = lax.rem(u, ring_b)
        a_copy(u).wait_recv()
        keep[i] = keep[i] + recv_a[lax.rem(u, ring_a), 0]
        send_b[i] = send_b[i] + recv_a[lax.rem(u, ring_a), 1]

        @pl.when(u < n_unit - ring_a)
        def _():
            pl.semaphore_signal(a_free, inc=1, device_id={'ep': core_peer}, device_id_type=MESH)

        @pl.when(u >= ring_b)
        def _():
            pl.semaphore_wait(b_free, 1)

        b_copy(u).start()

    def across_y(u):
        i = lax.rem(u, ring_b)
        b_copy(u).wait_recv()

        @pl.when(u >= ring_c)
        def _():
            c_copy(u - ring_c).wait_send()

        send_c[lax.rem(u, ring_c)] = (keep[i] + recv_b[i]).astype(BF16)
        c_copy(u).start()

        @pl.when(u < n_unit - ring_b)
        def _():
            pl.semaphore_signal(b_free, inc=1, device_id={'ep': x_peer}, device_id_type=MESH)

    pl.semaphore_wait(barrier, 3)
    ahead = nk - 2

    def phase_one(u, _):
        @pl.when(u < n_unit)
        def _():
            partial_sums(u)

        @pl.when(u >= 1)
        def _():
            across_x(u - 1)

        @pl.when((u >= 4) & (lax.rem(u, 2) == 0) & (u // 2 - 2 < ahead))
        def _():
            across_y(u // 2 - 2)

        return 0

    lax.fori_loop(0, n_unit + 1, phase_one, 0)

    def attend(hp):
        abuf[:, col(hp, bn)] = attend_heads(q_scr[...], k_scr[...], v_scr[...], seq_len)

    q_scr[...] = jnp.zeros_like(q_scr)
    k_scr[...] = jnp.zeros_like(k_scr)
    v_scr[...] = jnp.zeros_like(v_scr)
    n_under = n_hp // 2
    n_last = 3

    def finish(t):
        g, i = t // n_ot, lax.rem(t, ring_z)
        mine = pl.ds(pl.multiple_of(core * rows_g, rows_g), rows_g)
        z_copy(t).wait_recv()
        proj = (zscr[i, mine, :] + recv_z[lax.rem(t, ring_r)]).astype(BF16)

        @pl.when(t < 2 * n_ot - ring_r)
        def _():
            pl.semaphore_signal(z_free, inc=1, device_id={'ep': core_peer}, device_id_type=MESH)

        @pl.when(t >= ring_z)
        def _():
            out_copy(t - ring_z).wait()

        zout[i] = (y_own[g, :, col(lax.rem(t, n_ot), bn)].astype(F32) + proj.astype(F32)).astype(BF16)
        out_copy(t).start()

    def group_pass(g, _):
        def late(u, _):
            across_y(u)
            return 0

        lax.fori_loop(jnp.where(g == 0, ahead, n_unit - n_last), jnp.where(g == 0, nk, n_unit), late, 0)

        def arrived(k, _):
            c_copy(g * nk + k).wait_recv()
            return 0

        lax.fori_loop(0, nk, arrived, 0)

        def norm(p, _):
            for half in range(2):
                y = y_own[g, pl.ds(pl.multiple_of(p * 32 + half * 16, 16), 16), :].astype(F32)
                inv = lax.rsqrt(jnp.mean(y * y, axis=1, keepdims=True) + NORM_EPS)
                xbuf[g, pl.ds(pl.multiple_of(core * rows_g + p * 32 + half * 16, 16), 16), :] = (y * inv * nw_ref[...]).astype(BF16)
            x_copy(g, p).start()
            return 0

        lax.fori_loop(0, rows_g // 32, norm, 0)

        def exchanged(p, _):
            x_copy(g, p).wait()
            return 0

        lax.fori_loop(0, rows_g // 32, exchanged, 0)

        def heads(hp, _):
            s = g * n_tile + hp * 3
            for kind in range(3):
                qkv_tile(s + kind, hp, kind).wait()
            attend(jnp.maximum(hp - 1, 0))
            q = jnp.dot(xbuf[g], wbuf[lax.rem(s, n_w)], preferred_element_type=F32).astype(BF16)
            k = jnp.dot(xbuf[g], wbuf[lax.rem(s + 1, n_w)], preferred_element_type=F32).astype(BF16)
            v = jnp.dot(xbuf[g], wbuf[lax.rem(s + 2, n_w)], preferred_element_type=F32).astype(BF16)
            q_scr[...] = q
            k_scr[...] = k
            v_scr[...] = v
            for kind in range(3):
                start_tile(s + kind + n_w)

            @pl.when((g == 0) & (lax.rem(hp, 2) == 1))
            def _():
                across_y(nk + hp // 2)

            return 0

        lax.fori_loop(0, n_hp, heads, 0)
        attend(n_hp - 1)

        def project(i, _):
            for r in range(2):
                t = g * n_ot + 2 * i + r
                s = g * n_tile + 3 * n_hp + 2 * i + r

                @pl.when(t >= ring_z)
                def _():
                    z_copy(t - ring_z).wait_send()

                out_tile(s, 2 * i + r).wait()
            for r in range(2):
                t = g * n_ot + 2 * i + r
                s = g * n_tile + 3 * n_hp + 2 * i + r
                zscr[lax.rem(t, ring_z)] = jnp.dot(abuf[...], wbuf[lax.rem(s, n_w), 0:width, :], preferred_element_type=F32)
            for r in range(2):
                t = g * n_ot + 2 * i + r
                start_tile(g * n_tile + 3 * n_hp + 2 * i + r + n_w)

                @pl.when(t >= ring_r)
                def _():
                    pl.semaphore_wait(z_free, 1)

                z_copy(t).start()

            @pl.when(i >= 1)
            def _():
                finish(g * n_ot + 2 * i - 2)
                finish(g * n_ot + 2 * i - 1)

            @pl.when((g == 0) & (lax.rem(i, 5) == 2))
            def _():
                across_y(nk + n_under + i // 5)

            return 0

        lax.fori_loop(0, n_ot // 2, project, 0)
        finish(g * n_ot + n_ot - 2)
        finish(g * n_ot + n_ot - 1)
        return 0

    lax.fori_loop(0, 2, group_pass, 0)

    for u in range(n_unit - 2, n_unit):
        a_copy(u).wait_send()
    for u in range(n_unit - ring_b, n_unit):
        b_copy(u).wait_send()
    for u in range(n_unit - ring_c, n_unit):
        c_copy(u).wait_send()
    for t in range(2 * n_ot - ring_z, 2 * n_ot):
        z_copy(t).wait_send()
        out_copy(t).wait()


def stage(out_local, info, resid, norm_w, w_q, w_k, w_v, w_o, seq_len, n_ep, n_stages, dk=512, bn=256):
    n_exp, capacity, dim = out_local.shape
    n_tok = resid.shape[0]
    cap_dev = capacity // n_ep
    n_slot = n_exp * cap_dev
    width = w_q.shape[1] // 2
    rows_g = n_tok // 2
    n_unit = 2 * dim // dk
    n_w, ring_a, ring_b, ring_c, ring_z, ring_r = 6, 4, 16, 4, 4, 8
    any_spec = pl.BlockSpec(memory_space=pl.ANY)
    vmem_spec = pl.BlockSpec(memory_space=pltpu.VMEM)
    vmem, dma = pltpu.VMEM, pltpu.SemaphoreType.DMA
    return pl.pallas_call(
        functools.partial(stage_kernel, n_ep, n_stages, dk, bn, seq_len),
        out_shape=jax.ShapeDtypeStruct((n_tok, dim), BF16),
        in_specs=[any_spec, vmem_spec, any_spec, vmem_spec] + [any_spec] * 4,
        out_specs=any_spec,
        scratch_shapes=[
            vmem((n_ep, n_exp, cap_dev, dk), BF16),
            vmem((n_tok, dk), BF16),
            vmem((n_ep, 3 * rows_g, n_slot), BF16),
            vmem((rows_g, n_tok), BF16),
            vmem((2, 2, rows_g, dk), F32),
            vmem((ring_a, 2, rows_g, dk), F32),
            vmem((ring_b, rows_g, dk), F32),
            vmem((ring_b, rows_g, dk), F32),
            vmem((ring_b, rows_g, dk), F32),
            vmem((ring_c, rows_g, dk), BF16),
            vmem((2, rows_g, dim), BF16),
            vmem((2, n_tok, dim), BF16),
            vmem((n_w, dim, bn), BF16),
            vmem((n_tok, width), BF16),
            vmem((n_tok, bn), BF16), vmem((n_tok, bn), BF16), vmem((n_tok, bn), BF16),
            vmem((ring_z, n_tok, bn), F32),
            vmem((ring_r, rows_g, bn), F32),
            vmem((ring_z, rows_g, bn), BF16),
            dma((n_ep,)), dma((1,)), dma((2,)), dma((ring_a,)), dma((ring_b,)), dma((ring_b,)), dma((ring_c,)), dma((n_unit,)),
            dma((rows_g // 32,)), dma((2 * rows_g // 32,)), dma((n_w,)), dma((ring_z,)), dma((ring_r,)), dma((ring_z,)),
            pltpu.SemaphoreType.REGULAR, pltpu.SemaphoreType.REGULAR, pltpu.SemaphoreType.REGULAR,
        ],
        compiler_params=pltpu.CompilerParams(collective_id=0, has_side_effects=True, vmem_limit_bytes=VMEM_LIMIT),
        name='stage',
    )(out_local, info, resid, norm_w, w_q, w_k, w_v, w_o)


def attend_heads(q, k, v, seq_len, blk=128):
    n_tok, width = q.shape
    row = lax.broadcasted_iota(jnp.int32, (blk, blk), 0)
    col = lax.broadcasted_iota(jnp.int32, (blk, blk), 1)
    seen = (row >= col) & (row // seq_len == col // seq_len)
    heads = []
    for h in range(width // HEAD_DIM):
        tiles = []
        for t in range(n_tok // blk):
            at = (slice(t * blk, (t + 1) * blk), slice(h * HEAD_DIM, (h + 1) * HEAD_DIM))
            s = lax.dot_general(q[at], k[at], (((1,), (1,)), ((), ())), preferred_element_type=F32) * (HEAD_DIM ** -0.5)
            s = jnp.where(seen, s, -1e30)
            e = jnp.exp(s - jnp.max(s, axis=1, keepdims=True))
            p = (e / jnp.sum(e, axis=1, keepdims=True)).astype(BF16)
            tiles.append(jnp.dot(p, v[at], preferred_element_type=F32).astype(BF16))
        heads.append(jnp.concatenate(tiles, axis=0))
    return jnp.concatenate(heads, axis=1)


def place_kernel(src_ref, z_ref, out_ref):
    out_ref[...] = z_ref[...]


def place_sequences(src, z, seq_len):
    n_tok, dim = z.shape
    return pl.pallas_call(
        place_kernel,
        grid_spec=pltpu.PrefetchScalarGridSpec(
            num_scalar_prefetch=1,
            grid=(n_tok // seq_len,),
            in_specs=[pl.BlockSpec((seq_len, dim), lambda i, src: (src[i], 0))],
            out_specs=pl.BlockSpec((seq_len, dim), lambda i, src: (i, 0)),
        ),
        out_shape=jax.ShapeDtypeStruct((n_tok, dim), BF16),
        compiler_params=pltpu.CompilerParams(dimension_semantics=('arbitrary',)),
        name='place_sequences',
    )(src, z)


def arrival_order(owner_row, n_ep):
    seq_dev = owner_row.shape[0] // n_ep
    grid = owner_row.reshape(n_ep, seq_dev)
    key = (grid // seq_dev) * seq_dev + jnp.arange(seq_dev)
    place = jnp.sum(key[:, None, :] < key[:, :, None], axis=2)
    chosen = (place[:, None, :] == jnp.arange(seq_dev)[:, None]).astype(jnp.int32)
    return jnp.sum(chosen * grid[:, None, :], axis=2), place


def solution(mesh):
    n_stages = mesh.shape['pp']
    n_ep = mesh.shape['ep']
    group_axes = ('data', 'pp')

    def device_step(expert_out, expert_id, slot_id, gate, resid, owner, norm_w, w_q, w_k, w_v, w_o):
        me = lax.axis_index('ep')
        out_local, h = expert_out[0, 0], resid[0, 0]
        n_exp, capacity, dim = out_local.shape
        cap_dev = capacity // n_ep
        n_tok = h.shape[0]
        n_seq = owner.shape[1]
        seq_dev = n_seq // n_ep
        seq_len = n_tok // seq_dev
        n_slot = n_exp * cap_dev

        owner_next = lax.ppermute(owner[0], 'pp', [((r + 1) % n_stages, r) for r in range(n_stages)])
        ids, slots = expert_id[0, 0], slot_id[0, 0]
        index = jnp.where(slots >= 0, ids * cap_dev + slots - me * cap_dev, -1).astype(F32)
        local = jnp.broadcast_to(jnp.arange(n_tok, dtype=F32)[:, None], (n_tok, 1))
        table = lax.all_gather(jnp.concatenate([index, gate[0, 0], local], axis=1), 'ep', axis=0, tiled=True)
        dest_seqs, _ = arrival_order(owner_next, n_ep)
        relative = jnp.bitwise_xor(me, jnp.array([0, 2, 1, 3]))
        pick = dest_seqs[relative].reshape(n_ep, n_ep, seq_dev // n_ep).transpose(1, 2, 0).reshape(n_seq)
        info = table.reshape(n_seq, seq_len * 17)[pick].reshape(n_ep, n_tok, 17)
        info = jnp.concatenate([info[:, :, :8] - (me * n_slot).astype(F32), info[:, :, 8:]], axis=2)

        z = stage(out_local, info, h, norm_w, w_q[0], w_k[0], w_v[0], w_o[0], seq_len, n_ep, n_stages)

        _, places = arrival_order(owner[0], n_ep)
        place = lax.dynamic_index_in_dim(places, me, 0, keepdims=False)
        src = (place % 2 * n_ep + place // 2).astype(jnp.int32)
        return place_sequences(src, z, seq_len)[None, None]

    tok_spec = P(group_axes, None, 'ep', None)
    weight_spec = P('pp', None, None)
    in_specs = (P(group_axes, None, 'ep', None, None), tok_spec, tok_spec, tok_spec, tok_spec, P(group_axes, None), P('pp', None), weight_spec,
                weight_spec, weight_spec, weight_spec)
    return jax.shard_map(device_step, mesh=mesh, in_specs=in_specs, out_specs=tok_spec, check_vma=False)
```

time: 1060 us -> 328 us (0.31)
  waiting for transfers between devices: 591 us -> 0.01 us
  Pallas kernels: 0 us -> 307 us
  matrix products: 205 us -> 0 us
  local copies, waits for them, and re-layouts: 192 us -> 3.3 us
  other arithmetic: 44.7 us -> 5.6 us
  starting transfers between devices: 19.6 us -> 3.37 us
    all_to_all x2 -> x0, waiting for transfers between devices: 515 us -> none  [the longest x1 475 us: device_step(): recv_out = lax.all_to_all(out_local, 'ep', 2, 1, tiled=True)]
    pallas_call x0 -> x2, Pallas kernels: none -> 307 us  [the longest x1 300 us: stage(): pl.pallas_call(functools.partial(stage_kernel, n_ep, n_stages, dk, bn, se...]
    dot_general x6 -> x0, matrix products: 205 us -> none  [the longest x3 140 us: project(): jnp.einsum('msld,de->msle', normed, weight, preferred_element_type=jnp.fl...]
    gather x11 -> x3, local copies, waits for them, and re-layouts: 108 us -> 1.27 us  [the longest x2 0.65 us: device_step(): dest_seqs[relative].reshape(n_ep, n_ep, seq_dev // n_ep).transpose(1, 2, 0)]
    ppermute x1, waiting for transfers between devices: 76 us -> 0.01 us  [device_step(): lax.ppermute(owner[0], 'pp', [((r + 1) % n_stages, r) for r in range(n_st...]
    unnamed x16 -> x1, local copies, waits for them, and re-layouts: 43.4 us -> 0.51 us
    all_to_all x1 -> x0, local copies, waits for them, and re-layouts: 39.8 us -> none  [device_step(): recv_out = lax.all_to_all(out_local, 'ep', 2, 1, tiled=True)]
    reduce_sum x2 -> x3, other arithmetic: 26.4 us -> 0.58 us  [the longest x2 0.43 us: arrival_order(): place = jnp.sum(key[:, None, :] < key[:, :, None], axis=2)]
  transfers between devices with their start and end apart: 3 -> 1, of which waited for: 3 -> 0; matrix products, arithmetic and copies ran while one was open for 1% -> 2% of each run, Pallas kernels for 0% -> 0%
where the time goes in v2:
time: 328 us; the launch traced here: 327 us
  Pallas kernels  307 us (94%)
  blocking collectives  8.29 us (3%)
  other arithmetic  5.6 us (2%)
  starting transfers between devices  3.37 us (1%)
  local copies, waits for them, and re-layouts  3.3 us (1%)
    pallas_call x1, Pallas kernels, stage(): pl.pallas_call(functools.partial(stage_kernel, n_ep, n_stages, dk, bn, se...  300 us
    all_gather x1, blocking collectives, device_step(): lax.all_gather(jnp.concatenate([index, gate[0, 0], local], axis=1), 'ep',...  8.29 us
    pallas_call x1, Pallas kernels, place_sequences(): pl.pallas_call(place_kernel, grid_spec=pltpu.PrefetchScalarGridSpec(num_s...  7.03 us
  transfers between devices with their start and end apart: 1, of which 0 were waited for; matrix products, arithmetic and copies ran while one was open for 2% of the time, Pallas kernels for 0%

profile of v2, /device:TPU:0, one launch (start us, length us, event | category | flops | bytes accessed | tf_op | source)
XLA Modules:
  0.0 327.2 jit_solution(12167649985234647433)
XLA Ops:
  0.0 3.4 %collective-permute-start = (s32[32]{0:T(128)}, s32[32]{0:T(128)S(1)}, u32[]{:S(2)}, u32[]{:S(2)}) collective-permute-start(s32[32]{0:T(128)} %bitcast.33), channel_id=1, source_target_pairs={{4,0},{0,4},{5,1},{1,5},{6,2},{2,6},{7,3},{3,7}} | collective-permute-start | bytes 392 | tf_op jit(solution)/shard_map/ppermute | solution.py:464
  3.4 0.5 broadcast.211
  3.9 1.3 reduce.3
  5.2 0.7 compare_select_fusion.1
  5.9 0.1 reshape_squeeze.3
  6.0 0.2 convert_reduce_fusion.1
  6.2 0.7 convert_bitcast_fusion
  6.9 0.7 pad_maximum_fusion.1
  7.6 8.3 %all_gather.3 = f32[1024,17]{0,1:T(8,128)S(1)} all-gather(f32[256,17]{0,1:T(8,128)S(1)} %pad_maximum_fusion.1), channel_id=1, replica_groups=mesh['data'=1,'pp'=2,'ep'=4] {'ep'}, dimensions={0}, use_global_device_ids=true | all-gather | bytes 87040 | tf_op jit(solution)/shard_map/all_gather | solution.py:468
  15.9 0.5 fusion.9.src_ref
  16.4 0.2 copy.22
  16.7 0.3 reshape.194
  16.9 0.0 collective-permute-done
  16.9 0.1 reshape.195
  17.0 0.2 convert_reduce_fusion
  17.3 0.2 select_reduce_fusion
  17.4 0.6 gather_fusion
  18.0 0.1 copy.23
  18.1 0.1 reshape.197
  18.2 0.6 gather_fusion.1
  18.8 0.6 reshape.198
  19.4 0.2 slice.13
  19.6 1.0 pad_maximum_fusion.info_ref
  20.6 299.6 %stage.1.z_ref = bf16[256,7168]{1,0:T(8,128)(2,1)} custom-call(bf16[96,32,7168]{2,1,0:T(8,128)(2,1)} %bitcast.29, f32[4,256,17]{2,1,0:T(8,128)} %pad_maximum_fusion.info_ref, bf16[256,7168]{1,0:T(8,128)(2,1)} %bitcast.30, f32[1,7168]{1,0:T(1,128)} %nw_ref.1, bf16[7168,8192]{1,0:T(8,128)(2,1)} %bitcast.9.wq_hbm, bf16[7168,8192]{1,0:T(8,128)(2,1)} %bitcast.10.wk_hbm, ...), custom_call_target="tpu_custom_call" | custom-call | tf_op jit(solution)/shard_map/stage/pallas_call | solution.py:367
  320.2 7.0 %place_sequences.1 = bf16[256,7168]{1,0:T(8,128)(2,1)} custom-call(s32[8]{0:T(128)} %fusion.9.src_ref, bf16[256,7168]{1,0:T(8,128)(2,1)} %stage.1.z_ref), custom_call_target="tpu_custom_call" | custom-call | tf_op jit(solution)/shard_map/place_sequences/pallas_call | solution.py:425
  (7 shorter events, 0.1 us)
Async XLA Ops:
  0.0 16.9 %collective-permute-start = (s32[32]{0:T(128)}, s32[32]{0:T(128)S(1)}, u32[]{:S(2)}, u32[]{:S(2)}) collective-permute-start(s32[32]{0:T(128)} %bitcast.33), channel_id=1, source_target_pairs={{4,0},{0,4},{5,1},{1,5},{6,2},{2,6},{7,3},{3,7}} | collective-permute-start | bytes 392 | tf_op jit(solution)/shard_map/ppermute | solution.py:464

commit v3 on v2

--- a/solution.py
+++ b/solution.py
@@ -14,17 +14,16 @@
 VMEM_LIMIT = 66_000_000
 
 
-def stage_kernel(n_ep, n_stages, dk, bn, seq_len, o_hbm, info_ref, h_hbm, nw_ref, wq_hbm, wk_hbm, wv_hbm, wo_hbm, z_hbm, obuf, hbuf, w3, perm,
+def stage_kernel(n_ep, n_stages, dk, bn, seq_len, o_hbm, table_ref, meta_ref, h_hbm, nw_ref, wq_hbm, wk_hbm, wv_hbm, wo_hbm, z_hbm, tables, meta, obuf, hbuf, w3, perm,
                  send_a, recv_a, keep, send_b, recv_b, send_c, y_own, xbuf, wbuf, abuf, q_scr, k_scr, v_scr, zscr, recv_z, zout,
                  o_sem, h_sem, sa_sem, ra_sem, sb_sem, rb_sem, sc_sem, rc_sem, sx_sem, rx_sem, w_sem, sz_sem, rz_sem, out_sem,
-                 a_free, b_free, z_free):
+                 st_sem, rt_sem, sm_sem, rm_sem, a_free, b_free, z_free):
     me = lax.axis_index('ep')
     rank = lax.axis_index('pp')
     core = lax.rem(me, 2)
     core_peer = me + 1 - 2 * core
     x_peer = lax.rem(me + 2, n_ep)
-    next_rank = lax.rem(rank + 1, n_stages)
-    prev_rank = lax.rem(rank + n_stages - 1, n_stages)
+    other_rank = 1 - rank
     n_exp, cap_dev, n_slot = obuf.shape[1], obuf.shape[2], perm.shape[1] * 3
     n_tok, dim = h_hbm.shape
     n_slot = n_exp * cap_dev
@@ -62,7 +61,7 @@
     def c_copy(u):
         i = lax.rem(u, ring_c)
         return pltpu.make_async_remote_copy(send_c.at[i], y_own.at[u // nk, :, col(lax.rem(u, nk), dk)], sc_sem.at[i], rc_sem.at[u],
-                                            device_id={'pp': next_rank}, device_id_type=MESH)
+                                            device_id={'pp': other_rank}, device_id_type=MESH)
 
     def x_copy(g, p):
         at = xbuf.at[g, pl.ds(pl.multiple_of(core * rows_g + p * 32, 32), 32)]
@@ -104,32 +103,50 @@
     for o in range(n_ep):
         o_copy(0, o).start()
     h_copy(0).start()
-    for s in range(n_w):
-        qkv_tile(s, s // 3, s % 3).start()
-
     barrier = pltpu.get_barrier_semaphore()
-    pl.semaphore_signal(barrier, inc=1, device_id={'ep': core_peer}, device_id_type=MESH)
-    pl.semaphore_signal(barrier, inc=1, device_id={'ep': x_peer}, device_id_type=MESH)
-    pl.semaphore_signal(barrier, inc=1, device_id={'pp': prev_rank}, device_id_type=MESH)
+    for o in range(1, n_ep):
+        pl.semaphore_signal(barrier, inc=1, device_id={'ep': lax.rem(me + o, n_ep)}, device_id_type=MESH)
+    pl.semaphore_signal(barrier, inc=1, device_id={'pp': other_rank}, device_id_type=MESH)
+
+    def table_copy(o, source):
+        return pltpu.make_async_remote_copy(table_ref, tables.at[source], st_sem.at[o], rt_sem.at[source],
+                                            device_id={'ep': lax.rem(me + o, n_ep)}, device_id_type=MESH)
+
+    meta_copy = pltpu.make_async_remote_copy(meta_ref, meta, sm_sem.at[0], rm_sem.at[0], device_id={'pp': other_rank}, device_id_type=MESH)
 
     def build(g):
-        def block(step, _):
-            o = step // n_ep
-            part = lax.rem(step, n_ep) * sub
-            rows = info_ref[lax.rem(me + o, n_ep), pl.ds(pl.multiple_of(g * rows_g + part, sub), sub), :]
-            slot = lax.broadcasted_iota(jnp.int32, (sub, n_slot), 1).astype(F32)
-            w = jnp.zeros((sub, n_slot), F32)
-            for c in range(8):
-                w = jnp.where(rows[:, c:c + 1] == slot, rows[:, 8 + c:9 + c], w)
-            for t in range(3):
-                high = w.astype(BF16)
-                w3[o, pl.ds(pl.multiple_of(t * rows_g + part, sub), sub), :] = high
-                w = w - high.astype(F32)
-            return 0
-
-        lax.fori_loop(0, n_ep * n_ep, block, 0)
-        home = info_ref[me, pl.ds(pl.multiple_of(g * rows_g, rows_g), rows_g), 16:17]
-        perm[...] = (home == lax.broadcasted_iota(jnp.int32, (rows_g, n_tok), 1).astype(F32)).astype(F32).astype(BF16)
+        slot = lax.broadcasted_iota(jnp.int32, (sub, n_slot), 1).astype(F32) + (me * n_slot).astype(F32)
+        token = lax.broadcasted_iota(jnp.int32, (sub, n_tok), 1).astype(F32)
+        line = lax.broadcasted_iota(jnp.int32, (sub, 1), 0).astype(F32)
+
+        def block(o, _):
+            j = lax.rem(me + o, n_ep)
+            table = tables[j].T
+            code = meta[pl.ds(j, 1), :]
+            for r in range(n_ep):
+                dest = 2 * (me // 2) + core if r == 0 else 2 * (1 - me // 2) + core if r == 1 else 2 * (me // 2) + 1 - core if r == 2 else 2 * (1 - me // 2) + 1 - core
+                want = (2 * dest + g).astype(F32)
+                rows = jnp.zeros((sub, table.shape[1]), F32)
+                home = jnp.zeros((1, 1), F32)
+                for q in range(n_tok // sub):
+                    here = code[:, q:q + 1] == want
+                    rows = jnp.where(here, table[q * sub:(q + 1) * sub], rows)
+                    home = jnp.where(here, float(q * sub), home)
+                w = jnp.zeros((sub, n_slot), F32)
+                for c in range(8):
+                    w = jnp.where(rows[:, c:c + 1] == slot, rows[:, 8 + c:9 + c], w)
+                for t in range(3):
+                    high = w.astype(BF16)
+                    w3[o, t * rows_g + r * sub:t * rows_g + (r + 1) * sub, :] = high
+                    w = w - high.astype(F32)
+
+                @pl.when(o == 0)
+                def _():
+                    perm[r * sub:(r + 1) * sub, :] = (home + line == token).astype(F32).astype(BF16)
+
+            return 0
+
+        lax.fori_loop(0, n_ep, block, 0)
 
     def partial_sums(u):
         @pl.when(lax.rem(u, nk) == 0)
@@ -201,7 +218,14 @@
         def _():
             pl.semaphore_signal(b_free, inc=1, device_id={'ep': x_peer}, device_id_type=MESH)
 
-    pl.semaphore_wait(barrier, 3)
+    pl.semaphore_wait(barrier, n_ep)
+    meta_copy.start()
+    for o in range(1, n_ep):
+        table_copy(o, me).start()
+    tables[me] = table_ref[...]
+    meta_copy.wait_recv()
+    for o in range(1, n_ep):
+        table_copy(o, lax.rem(me + o, n_ep)).wait_recv()
     ahead = nk - 2
 
     def phase_one(u, _):
@@ -209,6 +233,10 @@
         def _():
             partial_sums(u)
 
+        @pl.when((u >= 2) & (u < 2 + n_w))
+        def _():
+            start_tile(u - 2)
+
         @pl.when(u >= 1)
         def _():
             across_x(u - 1)
@@ -222,13 +250,16 @@
     lax.fori_loop(0, n_unit + 1, phase_one, 0)
 
     def attend(hp):
-        abuf[:, col(hp, bn)] = attend_heads(q_scr[...], k_scr[...], v_scr[...], seq_len)
+        abuf[:, col(hp, bn)] = head_mix(head_probs(head_scores(q_scr[...], k_scr[...]), seq_len), v_scr[...])
 
     q_scr[...] = jnp.zeros_like(q_scr)
     k_scr[...] = jnp.zeros_like(k_scr)
     v_scr[...] = jnp.zeros_like(v_scr)
-    n_under = n_hp // 2
-    n_last = 3
+
+    def under(hp):
+        return (hp + 1) * 3 // 5 if isinstance(hp, int) else lax.div((hp + 1) * 3, 5)
+
+    n_last = max(0, nk - under(n_hp - 1) - (n_ot // 2 + 2) // 3)
 
     def finish(t):
         g, i = t // n_ot, lax.rem(t, ring_z)
@@ -280,19 +311,21 @@
             s = g * n_tile + hp * 3
             for kind in range(3):
                 qkv_tile(s + kind, hp, kind).wait()
-            attend(jnp.maximum(hp - 1, 0))
+            scores = head_scores(q_scr[...], k_scr[...])
             q = jnp.dot(xbuf[g], wbuf[lax.rem(s, n_w)], preferred_element_type=F32).astype(BF16)
+            mixed = head_mix(head_probs(scores, seq_len), v_scr[...])
             k = jnp.dot(xbuf[g], wbuf[lax.rem(s + 1, n_w)], preferred_element_type=F32).astype(BF16)
             v = jnp.dot(xbuf[g], wbuf[lax.rem(s + 2, n_w)], preferred_element_type=F32).astype(BF16)
+            abuf[:, col(jnp.maximum(hp - 1, 0), bn)] = mixed
             q_scr[...] = q
             k_scr[...] = k
             v_scr[...] = v
             for kind in range(3):
                 start_tile(s + kind + n_w)
 
-            @pl.when((g == 0) & (lax.rem(hp, 2) == 1))
+            @pl.when((g == 0) & (under(hp) > under(hp - 1)))
             def _():
-                across_y(nk + hp // 2)
+                across_y(nk + under(hp) - 1)
 
             return 0
 
@@ -328,9 +361,9 @@
                 finish(g * n_ot + 2 * i - 2)
                 finish(g * n_ot + 2 * i - 1)
 
-            @pl.when((g == 0) & (lax.rem(i, 5) == 2))
+            @pl.when((g == 0) & (lax.rem(i, 3) == 0) & (under(n_hp - 1) + i // 3 < nk))
             def _():
-                across_y(nk + n_under + i // 5)
+                across_y(nk + under(n_hp - 1) + i // 3)
 
             return 0
 
@@ -341,6 +374,9 @@
 
     lax.fori_loop(0, 2, group_pass, 0)
 
+    meta_copy.wait_send()
+    for o in range(1, n_ep):
+        table_copy(o, me).wait_send()
     for u in range(n_unit - 2, n_unit):
         a_copy(u).wait_send()
     for u in range(n_unit - ring_b, n_unit):
@@ -352,7 +388,7 @@
         out_copy(t).wait()
 
 
-def stage(out_local, info, resid, norm_w, w_q, w_k, w_v, w_o, seq_len, n_ep, n_stages, dk=512, bn=256):
+def stage(out_local, table, meta, resid, norm_w, w_q, w_k, w_v, w_o, seq_len, n_ep, n_stages, dk=512, bn=256):
     n_exp, capacity, dim = out_local.shape
     n_tok = resid.shape[0]
     cap_dev = capacity // n_ep
@@ -367,9 +403,11 @@
     return pl.pallas_call(
         functools.partial(stage_kernel, n_ep, n_stages, dk, bn, seq_len),
         out_shape=jax.ShapeDtypeStruct((n_tok, dim), BF16),
-        in_specs=[any_spec, vmem_spec, any_spec, vmem_spec] + [any_spec] * 4,
+        in_specs=[any_spec, vmem_spec, vmem_spec, any_spec, vmem_spec] + [any_spec] * 4,
         out_specs=any_spec,
         scratch_shapes=[
+            vmem((n_ep,) + table.shape, F32),
+            vmem(meta.shape, F32),
             vmem((n_ep, n_exp, cap_dev, dk), BF16),
             vmem((n_tok, dk), BF16),
             vmem((n_ep, 3 * rows_g, n_slot), BF16),
@@ -390,93 +428,104 @@
             vmem((ring_z, rows_g, bn), BF16),
             dma((n_ep,)), dma((1,)), dma((2,)), dma((ring_a,)), dma((ring_b,)), dma((ring_b,)), dma((ring_c,)), dma((n_unit,)),
             dma((rows_g // 32,)), dma((2 * rows_g // 32,)), dma((n_w,)), dma((ring_z,)), dma((ring_r,)), dma((ring_z,)),
+            dma((n_ep,)), dma((n_ep,)), dma((1,)), dma((1,)),
             pltpu.SemaphoreType.REGULAR, pltpu.SemaphoreType.REGULAR, pltpu.SemaphoreType.REGULAR,
         ],
         compiler_params=pltpu.CompilerParams(collective_id=0, has_side_effects=True, vmem_limit_bytes=VMEM_LIMIT),
         name='stage',
-    )(out_local, info, resid, norm_w, w_q, w_k, w_v, w_o)
-
-
-def attend_heads(q, k, v, seq_len, blk=128):
-    n_tok, width = q.shape
+    )(out_local, table, meta, resid, norm_w, w_q, w_k, w_v, w_o)
+
+
+def head_tiles(n_tok, width, blk):
+    return [(slice(t * blk, (t + 1) * blk), slice(h * HEAD_DIM, (h + 1) * HEAD_DIM)) for h in range(width // HEAD_DIM) for t in range(n_tok // blk)]
+
+
+def head_scores(q, k, blk=128):
+    return [lax.dot_general(q[at], k[at], (((1,), (1,)), ((), ())), preferred_element_type=F32) for at in head_tiles(*q.shape, blk)]
+
+
+def head_probs(scores, seq_len):
+    blk = scores[0].shape[0]
     row = lax.broadcasted_iota(jnp.int32, (blk, blk), 0)
     col = lax.broadcasted_iota(jnp.int32, (blk, blk), 1)
     seen = (row >= col) & (row // seq_len == col // seq_len)
-    heads = []
-    for h in range(width // HEAD_DIM):
-        tiles = []
-        for t in range(n_tok // blk):
-            at = (slice(t * blk, (t + 1) * blk), slice(h * HEAD_DIM, (h + 1) * HEAD_DIM))
-            s = lax.dot_general(q[at], k[at], (((1,), (1,)), ((), ())), preferred_element_type=F32) * (HEAD_DIM ** -0.5)
-            s = jnp.where(seen, s, -1e30)
-            e = jnp.exp(s - jnp.max(s, axis=1, keepdims=True))
-            p = (e / jnp.sum(e, axis=1, keepdims=True)).astype(BF16)
-            tiles.append(jnp.dot(p, v[at], preferred_element_type=F32).astype(BF16))
-        heads.append(jnp.concatenate(tiles, axis=0))
-    return jnp.concatenate(heads, axis=1)
-
-
-def place_kernel(src_ref, z_ref, out_ref):
-    out_ref[...] = z_ref[...]
+    probs = []
+    for s in scores:
+        s = jnp.where(seen, s * (HEAD_DIM ** -0.5), -1e30)
+        e = jnp.exp(s - jnp.max(s, axis=1, keepdims=True))
+        probs.append((e / jnp.sum(e, axis=1, keepdims=True)).astype(BF16))
+    return probs
+
+
+def head_mix(probs, v):
+    n_tok, width = v.shape
+    blk = probs[0].shape[0]
+    tiles = [jnp.dot(p, v[at], preferred_element_type=F32).astype(BF16) for p, at in zip(probs, head_tiles(n_tok, width, blk))]
+    per_head = n_tok // blk
+    return jnp.concatenate([jnp.concatenate(tiles[h * per_head:(h + 1) * per_head], axis=0) for h in range(width // HEAD_DIM)], axis=1)
+
+
+def place_kernel(seq_len, src_ref, z_hbm, out_hbm, buf, in_sem, out_sem):
+    n_seq = buf.shape[0]
+
+    def take(b):
+        return pltpu.make_async_copy(z_hbm.at[pl.ds(pl.multiple_of(src_ref[b] * seq_len, seq_len), seq_len)], buf.at[b], in_sem.at[b])
+
+    def put(b):
+        return pltpu.make_async_copy(buf.at[b], out_hbm.at[pl.ds(b * seq_len, seq_len)], out_sem.at[b])
+
+    for b in range(n_seq):
+        take(b).start()
+    for b in range(n_seq):
+        take(b).wait()
+        put(b).start()
+    for b in range(n_seq):
+        put(b).wait()
 
 
 def place_sequences(src, z, seq_len):
     n_tok, dim = z.shape
+    n_seq = n_tok // seq_len
     return pl.pallas_call(
-        place_kernel,
-        grid_spec=pltpu.PrefetchScalarGridSpec(
-            num_scalar_prefetch=1,
-            grid=(n_tok // seq_len,),
-            in_specs=[pl.BlockSpec((seq_len, dim), lambda i, src: (src[i], 0))],
-            out_specs=pl.BlockSpec((seq_len, dim), lambda i, src: (i, 0)),
-        ),
+        functools.partial(place_kernel, seq_len),
+        in_specs=[pl.BlockSpec(memory_space=pltpu.SMEM), pl.BlockSpec(memory_space=pl.ANY)],
+        out_specs=pl.BlockSpec(memory_space=pl.ANY),
         out_shape=jax.ShapeDtypeStruct((n_tok, dim), BF16),
-        compiler_params=pltpu.CompilerParams(dimension_semantics=('arbitrary',)),
+        scratch_shapes=[pltpu.VMEM((n_seq, seq_len, dim), BF16), pltpu.SemaphoreType.DMA((n_seq,)), pltpu.SemaphoreType.DMA((n_seq,))],
         name='place_sequences',
     )(src, z)
-
-
-def arrival_order(owner_row, n_ep):
-    seq_dev = owner_row.shape[0] // n_ep
-    grid = owner_row.reshape(n_ep, seq_dev)
-    key = (grid // seq_dev) * seq_dev + jnp.arange(seq_dev)
-    place = jnp.sum(key[:, None, :] < key[:, :, None], axis=2)
-    chosen = (place[:, None, :] == jnp.arange(seq_dev)[:, None]).astype(jnp.int32)
-    return jnp.sum(chosen * grid[:, None, :], axis=2), place
 
 
 def solution(mesh):
     n_stages = mesh.shape['pp']
     n_ep = mesh.shape['ep']
+    assert n_stages == 2 and n_ep == 4
     group_axes = ('data', 'pp')
 
     def device_step(expert_out, expert_id, slot_id, gate, resid, owner, norm_w, w_q, w_k, w_v, w_o):
         me = lax.axis_index('ep')
         out_local, h = expert_out[0, 0], resid[0, 0]
-        n_exp, capacity, dim = out_local.shape
-        cap_dev = capacity // n_ep
+        cap_dev = out_local.shape[1] // n_ep
         n_tok = h.shape[0]
         n_seq = owner.shape[1]
         seq_dev = n_seq // n_ep
         seq_len = n_tok // seq_dev
-        n_slot = n_exp * cap_dev
-
-        owner_next = lax.ppermute(owner[0], 'pp', [((r + 1) % n_stages, r) for r in range(n_stages)])
-        ids, slots = expert_id[0, 0], slot_id[0, 0]
+
+        ids, slots = expert_id[0, 0].T, slot_id[0, 0].T
         index = jnp.where(slots >= 0, ids * cap_dev + slots - me * cap_dev, -1).astype(F32)
-        local = jnp.broadcast_to(jnp.arange(n_tok, dtype=F32)[:, None], (n_tok, 1))
-        table = lax.all_gather(jnp.concatenate([index, gate[0, 0], local], axis=1), 'ep', axis=0, tiled=True)
-        dest_seqs, _ = arrival_order(owner_next, n_ep)
-        relative = jnp.bitwise_xor(me, jnp.array([0, 2, 1, 3]))
-        pick = dest_seqs[relative].reshape(n_ep, n_ep, seq_dev // n_ep).transpose(1, 2, 0).reshape(n_seq)
-        info = table.reshape(n_seq, seq_len * 17)[pick].reshape(n_ep, n_tok, 17)
-        info = jnp.concatenate([info[:, :, :8] - (me * n_slot).astype(F32), info[:, :, 8:]], axis=2)
-
-        z = stage(out_local, info, h, norm_w, w_q[0], w_k[0], w_v[0], w_o[0], seq_len, n_ep, n_stages)
-
-        _, places = arrival_order(owner[0], n_ep)
-        place = lax.dynamic_index_in_dim(places, me, 0, keepdims=False)
-        src = (place % 2 * n_ep + place // 2).astype(jnp.int32)
+        table = jnp.concatenate([index, gate[0, 0].T], axis=0)
+
+        owned = owner[0].reshape(n_ep, seq_dev)
+        sender = owned // seq_dev
+        rows = jnp.arange(seq_dev)
+        second = jnp.sum((sender[:, :, None] == sender[:, None, :]) & (rows[None, :] < rows[:, None]), axis=2)
+        code = (2 * jnp.arange(n_ep)[:, None] + second).reshape(n_seq)
+        meta = jnp.sum(jnp.where(owner[0][None, :] == jnp.arange(n_seq)[:, None], code[None, :], 0), axis=1).astype(F32)
+        meta = jnp.pad(meta.reshape(n_ep, seq_dev), ((0, 8 - n_ep), (0, 128 - seq_dev)), constant_values=-1)
+
+        z = stage(out_local, table, meta, h, norm_w, w_q[0], w_k[0], w_v[0], w_o[0], seq_len, n_ep, n_stages)
+
+        src = lax.dynamic_index_in_dim(second * n_ep + sender, me, 0, keepdims=False).astype(jnp.int32)
         return place_sequences(src, z, seq_len)[None, None]
 
     tok_spec = P(group_axes, None, 'ep', None)

time: 328 us -> 285 us (0.87)
  Pallas kernels: 307 us -> 279 us
  blocking collectives: 8.29 us -> 0 us
  starting transfers between devices: 3.37 us -> 0 us
    pallas_call x1, Pallas kernels: 300 us -> 275 us  [stage(): pl.pallas_call(functools.partial(stage_kernel, n_ep, n_stages, dk, bn, se...]
    all_gather x1 -> x0, blocking collectives: 8.29 us -> none  [device_step(): lax.all_gather(jnp.concatenate([index, gate[0, 0], local], axis=1), 'ep',...]
    ppermute x1 -> x0, starting transfers between devices: 3.37 us -> none  [device_step(): lax.ppermute(owner[0], 'pp', [((r + 1) % n_stages, r) for r in range(n_st...]
    pallas_call x1, Pallas kernels: 7.03 us -> 3.73 us  [place_sequences(): pl.pallas_call(functools.partial(place_kernel, seq_len), in_specs=[pl.Blo...]
  transfers between devices with their start and end apart: 1 -> 0, of which waited for: 0 -> 0; matrix products, arithmetic and copies ran while one was open for 2% -> 0% of each run, Pallas kernels for 0% -> 0%
where the time goes in v3:
time: 285 us
  Pallas kernels  279 us (98%)
  other arithmetic  4.43 us (2%)
    pallas_call x1, Pallas kernels, stage(): pl.pallas_call(functools.partial(stage_kernel, n_ep, n_stages, dk, bn, se...  275 us

profile of v3, /device:TPU:0, one launch (start us, length us, event | category | flops | bytes accessed | tf_op | source)
XLA Modules:
  0.0 285.0 jit_solution(14140464701894976253)
XLA Ops:
  0.0 0.5 broadcast.98
  0.5 1.3 reduce.3
  1.8 0.1 reshape_squeeze.3
  1.9 0.2 convert_reduce_fusion
  2.2 0.1 broadcast_add_fusion
  2.2 0.1 add.43
  2.3 0.8 select_reduce_fusion
  3.1 0.6 dynamic-slice_bitcast_fusion.src_ref
  3.7 0.1 convert_element_type.18
  3.8 0.6 pad.4.meta_ref
  4.4 0.7 convert_bitcast_fusion
  5.1 1.3 pad_maximum_fusion.table_ref
  6.4 274.9 %stage.1.z_hbm = bf16[256,7168]{1,0:T(8,128)(2,1)} custom-call(bf16[96,32,7168]{2,1,0:T(8,128)(2,1)} %bitcast.17, f32[16,256]{1,0:T(8,128)} %pad_maximum_fusion.table_ref, f32[8,128]{1,0:T(8,128)} %pad.4.meta_ref, bf16[256,7168]{1,0:T(8,128)(2,1)} %bitcast.18, f32[1,7168]{1,0:T(1,128)} %nw_ref.1, bf16[7168,8192]{1,0:T(8,128)(2,1)} %bitcast.8.wq_hbm, ...), custom_call_target="tpu_custom_call" | custom-call | tf_op jit(solution)/shard_map/stage/pallas_call | solution.py:403
  281.3 3.7 %place_sequences.1 = bf16[256,7168]{1,0:T(8,128)(2,1)} custom-call(s32[8]{0:T(128)} %dynamic-slice_bitcast_fusion.src_ref, bf16[256,7168]{1,0:T(8,128)(2,1)} %stage.1.z_hbm), custom_call_target="tpu_custom_call" | custom-call | tf_op jit(solution)/shard_map/place_sequences/pallas_call | solution.py:489
  (4 shorter events, 0.0 us)

commit v4 on v3

--- a/solution.py
+++ b/solution.py
@@ -11,10 +11,10 @@
 NORM_EPS = 1e-6
 F32, BF16 = jnp.float32, jnp.bfloat16
 MESH = pl.DeviceIdType.MESH
-VMEM_LIMIT = 66_000_000
-
-
-def stage_kernel(n_ep, n_stages, dk, bn, seq_len, o_hbm, table_ref, meta_ref, h_hbm, nw_ref, wq_hbm, wk_hbm, wv_hbm, wo_hbm, z_hbm, tables, meta, obuf, hbuf, w3, perm,
+VMEM_LIMIT = 67_043_328
+
+
+def stage_kernel(n_ep, n_stages, dk, bn, seq_len, o_hbm, ids_ref, slots_ref, gate_ref, own_ref, h_hbm, nw_ref, wq_hbm, wk_hbm, wv_hbm, wo_hbm, z_hbm, table_mine, meta_mine, tables, meta, obuf, hbuf, w3, perm,
                  send_a, recv_a, keep, send_b, recv_b, send_c, y_own, xbuf, wbuf, abuf, q_scr, k_scr, v_scr, zscr, recv_z, zout,
                  o_sem, h_sem, sa_sem, ra_sem, sb_sem, rb_sem, sc_sem, rc_sem, sx_sem, rx_sem, w_sem, sz_sem, rz_sem, out_sem,
                  st_sem, rt_sem, sm_sem, rm_sem, a_free, b_free, z_free):
@@ -109,59 +109,82 @@
     pl.semaphore_signal(barrier, inc=1, device_id={'pp': other_rank}, device_id_type=MESH)
 
     def table_copy(o, source):
-        return pltpu.make_async_remote_copy(table_ref, tables.at[source], st_sem.at[o], rt_sem.at[source],
+        return pltpu.make_async_remote_copy(table_mine, tables.at[source], st_sem.at[o], rt_sem.at[source],
                                             device_id={'ep': lax.rem(me + o, n_ep)}, device_id_type=MESH)
 
-    meta_copy = pltpu.make_async_remote_copy(meta_ref, meta, sm_sem.at[0], rm_sem.at[0], device_id={'pp': other_rank}, device_id_type=MESH)
-
-    def build(g):
+    meta_copy = pltpu.make_async_remote_copy(meta_mine, meta, sm_sem.at[0], rm_sem.at[0], device_id={'pp': other_rank}, device_id_type=MESH)
+
+    def tabulate():
+        slots = slots_ref[...]
+        table_mine[0:8, :] = jnp.where(slots >= 0, ids_ref[...] * cap_dev + slots - me * cap_dev, -1).astype(F32)
+        table_mine[8:16, :] = gate_ref[...]
+        n_seq = own_ref.shape[1]
+        seq_dev = n_seq // n_ep
+        down = lax.broadcasted_iota(jnp.int32, (n_seq, n_seq), 0)
+        across = lax.broadcasted_iota(jnp.int32, (n_seq, n_seq), 1)
+
+        def part(x):
+            return sum((x >= seq_dev * d).astype(F32) for d in range(1, n_ep))
+
+        own = jnp.broadcast_to(own_ref[...], (n_seq, n_seq)).astype(F32)
+        own_down = jnp.sum(jnp.where(down == across, own, 0.0), axis=1, keepdims=True)
+        earlier = (part(own_down) == part(own)) & (down < across) & (part(down) == part(across))
+        second = jnp.sum(earlier.astype(F32), axis=0, keepdims=True)
+        code = 2 * part(across) + second
+        code = jnp.sum(jnp.where(own == down.astype(F32), code, 0.0), axis=1, keepdims=True)
+        meta_mine[...] = jnp.broadcast_to(code, meta_mine.shape)
+
+    def build(g, o):
+        j = lax.rem(me + o, n_ep)
         slot = lax.broadcasted_iota(jnp.int32, (sub, n_slot), 1).astype(F32) + (me * n_slot).astype(F32)
-        token = lax.broadcasted_iota(jnp.int32, (sub, n_tok), 1).astype(F32)
-        line = lax.broadcasted_iota(jnp.int32, (sub, 1), 0).astype(F32)
-
-        def block(o, _):
-            j = lax.rem(me + o, n_ep)
-            table = tables[j].T
-            code = meta[pl.ds(j, 1), :]
-            for r in range(n_ep):
-                dest = 2 * (me // 2) + core if r == 0 else 2 * (1 - me // 2) + core if r == 1 else 2 * (me // 2) + 1 - core if r == 2 else 2 * (1 - me // 2) + 1 - core
-                want = (2 * dest + g).astype(F32)
-                rows = jnp.zeros((sub, table.shape[1]), F32)
-                home = jnp.zeros((1, 1), F32)
-                for q in range(n_tok // sub):
-                    here = code[:, q:q + 1] == want
-                    rows = jnp.where(here, table[q * sub:(q + 1) * sub], rows)
-                    home = jnp.where(here, float(q * sub), home)
-                w = jnp.zeros((sub, n_slot), F32)
-                for c in range(8):
-                    w = jnp.where(rows[:, c:c + 1] == slot, rows[:, 8 + c:9 + c], w)
-                for t in range(3):
-                    high = w.astype(BF16)
-                    w3[o, t * rows_g + r * sub:t * rows_g + (r + 1) * sub, :] = high
-                    w = w - high.astype(F32)
-
-                @pl.when(o == 0)
+        table = tables[j].T
+        wide = (sub, table.shape[1])
+        n_q = n_tok // sub
+        block = meta[pl.ds(pl.multiple_of(j * n_q, n_q), n_q), :]
+        codes = [jnp.broadcast_to(block[q:q + 1, :wide[1]], wide) for q in range(n_q)]
+        x_me = me // 2
+        for r in range(n_ep):
+            dest = 2 * (x_me if r % 2 == 0 else 1 - x_me) + (core if r < 2 else 1 - core)
+            want = (2 * dest + g).astype(F32)
+            rows = jnp.zeros(wide, F32)
+            for q in range(n_q):
+                rows = jnp.where(codes[q] == want, table[q * sub:(q + 1) * sub], rows)
+            w = jnp.zeros((sub, n_slot), F32)
+            for c in range(8):
+                w = jnp.where(rows[:, c:c + 1] == slot, rows[:, 8 + c:9 + c], w)
+            for t in range(3):
+                high = w.astype(BF16)
+                w3[o, t * rows_g + r * sub:t * rows_g + (r + 1) * sub, :] = high
+                w = w - high.astype(F32)
+            if o == 0:
+                home = jnp.zeros(wide, F32)
+                for q in range(n_q):
+                    home = jnp.where(codes[q] == want, float(q * sub), home)
+                token = lax.broadcasted_iota(jnp.int32, (sub, n_tok), 1)
+                line = lax.broadcasted_iota(jnp.int32, (sub, n_tok), 0)
+                perm[r * sub:(r + 1) * sub, :] = (home[:, 0:1] == (token - line).astype(F32)).astype(F32).astype(BF16)
+
+    def partial_sums(u):
+        @pl.when(u >= 2)
+        def _():
+            a_copy(u - 2).wait_send()
+
+        @pl.when(u >= ring_b)
+        def _():
+            b_copy(u - ring_b).wait_send()
+
+        for o in range(n_ep):
+            @pl.when(lax.rem(u, nk) == 0)
+            def _():
+                @pl.when(u == 0)
                 def _():
-                    perm[r * sub:(r + 1) * sub, :] = (home + line == token).astype(F32).astype(BF16)
-
-            return 0
-
-        lax.fori_loop(0, n_ep, block, 0)
-
-    def partial_sums(u):
-        @pl.when(lax.rem(u, nk) == 0)
-        def _():
-            build(u // nk)
-
-        @pl.when(u >= 2)
-        def _():
-            a_copy(u - 2).wait_send()
-
-        @pl.when(u >= ring_b)
-        def _():
-            b_copy(u - ring_b).wait_send()
-
-        for o in range(n_ep):
+                    if o == 0:
+                        meta_copy.wait_recv()
+                    else:
+                        table_copy(o, lax.rem(me + o, n_ep)).wait_recv()
+
+                build(u // nk, o)
+
             o_copy(u, o).wait()
             rows = obuf[o].reshape(n_slot, dk)
             split = jnp.dot(w3[o], rows, preferred_element_type=F32)
@@ -218,15 +241,13 @@
         def _():
             pl.semaphore_signal(b_free, inc=1, device_id={'ep': x_peer}, device_id_type=MESH)
 
+    tabulate()
     pl.semaphore_wait(barrier, n_ep)
     meta_copy.start()
     for o in range(1, n_ep):
         table_copy(o, me).start()
-    tables[me] = table_ref[...]
-    meta_copy.wait_recv()
-    for o in range(1, n_ep):
-        table_copy(o, lax.rem(me + o, n_ep)).wait_recv()
-    ahead = nk - 2
+    tables[me] = table_mine[...]
+    ahead = nk
 
     def phase_one(u, _):
         @pl.when(u < n_unit)
@@ -241,9 +262,9 @@
         def _():
             across_x(u - 1)
 
-        @pl.when((u >= 4) & (lax.rem(u, 2) == 0) & (u // 2 - 2 < ahead))
-        def _():
-            across_y(u // 2 - 2)
+        @pl.when((u >= 2) & (lax.rem(u, 2) == 0))
+        def _():
+            across_y(u // 2 - 1)
 
         return 0
 
@@ -388,7 +409,7 @@
         out_copy(t).wait()
 
 
-def stage(out_local, table, meta, resid, norm_w, w_q, w_k, w_v, w_o, seq_len, n_ep, n_stages, dk=512, bn=256):
+def stage(out_local, ids, slots, gate, owner, resid, norm_w, w_q, w_k, w_v, w_o, seq_len, n_ep, n_stages, dk=512, bn=256):
     n_exp, capacity, dim = out_local.shape
     n_tok = resid.shape[0]
     cap_dev = capacity // n_ep
@@ -396,18 +417,20 @@
     width = w_q.shape[1] // 2
     rows_g = n_tok // 2
     n_unit = 2 * dim // dk
-    n_w, ring_a, ring_b, ring_c, ring_z, ring_r = 6, 4, 16, 4, 4, 8
+    n_w, ring_a, ring_b, ring_c, ring_z, ring_r = 7, 3, 15, 2, 4, 4
     any_spec = pl.BlockSpec(memory_space=pl.ANY)
     vmem_spec = pl.BlockSpec(memory_space=pltpu.VMEM)
     vmem, dma = pltpu.VMEM, pltpu.SemaphoreType.DMA
     return pl.pallas_call(
         functools.partial(stage_kernel, n_ep, n_stages, dk, bn, seq_len),
         out_shape=jax.ShapeDtypeStruct((n_tok, dim), BF16),
-        in_specs=[any_spec, vmem_spec, vmem_spec, any_spec, vmem_spec] + [any_spec] * 4,
+        in_specs=[any_spec, vmem_spec, vmem_spec, vmem_spec, vmem_spec, any_spec, vmem_spec] + [any_spec] * 4,
         out_specs=any_spec,
         scratch_shapes=[
-            vmem((n_ep,) + table.shape, F32),
-            vmem(meta.shape, F32),
+            vmem((2 * ids.shape[0], n_tok), F32),
+            vmem((owner.shape[1], 128), F32),
+            vmem((n_ep, 2 * ids.shape[0], n_tok), F32),
+            vmem((owner.shape[1], 128), F32),
             vmem((n_ep, n_exp, cap_dev, dk), BF16),
             vmem((n_tok, dk), BF16),
             vmem((n_ep, 3 * rows_g, n_slot), BF16),
@@ -433,7 +456,7 @@
         ],
         compiler_params=pltpu.CompilerParams(collective_id=0, has_side_effects=True, vmem_limit_bytes=VMEM_LIMIT),
         name='stage',
-    )(out_local, table, meta, resid, norm_w, w_q, w_k, w_v, w_o)
+    )(out_local, ids, slots, gate, owner, resid, norm_w, w_q, w_k, w_v, w_o)
 
 
 def head_tiles(n_tok, width, blk):
@@ -465,11 +488,15 @@
     return jnp.concatenate([jnp.concatenate(tiles[h * per_head:(h + 1) * per_head], axis=0) for h in range(width // HEAD_DIM)], axis=1)
 
 
-def place_kernel(seq_len, src_ref, z_hbm, out_hbm, buf, in_sem, out_sem):
+def place_kernel(seq_len, n_ep, own_ref, z_hbm, out_hbm, buf, in_sem, out_sem):
     n_seq = buf.shape[0]
+    me = lax.axis_index('ep')
+    sender = [own_ref[0, me * n_seq + b] // n_seq for b in range(n_seq)]
 
     def take(b):
-        return pltpu.make_async_copy(z_hbm.at[pl.ds(pl.multiple_of(src_ref[b] * seq_len, seq_len), seq_len)], buf.at[b], in_sem.at[b])
+        second = sum([(sender[a] == sender[b]).astype(jnp.int32) for a in range(b)], jnp.int32(0))
+        row = pl.multiple_of((second * n_ep + sender[b]) * seq_len, seq_len)
+        return pltpu.make_async_copy(z_hbm.at[pl.ds(row, seq_len)], buf.at[b], in_sem.at[b])
 
     def put(b):
         return pltpu.make_async_copy(buf.at[b], out_hbm.at[pl.ds(b * seq_len, seq_len)], out_sem.at[b])
@@ -483,17 +510,17 @@
         put(b).wait()
 
 
-def place_sequences(src, z, seq_len):
+def place_sequences(owner, z, seq_len, n_ep):
     n_tok, dim = z.shape
     n_seq = n_tok // seq_len
     return pl.pallas_call(
-        functools.partial(place_kernel, seq_len),
+        functools.partial(place_kernel, seq_len, n_ep),
         in_specs=[pl.BlockSpec(memory_space=pltpu.SMEM), pl.BlockSpec(memory_space=pl.ANY)],
         out_specs=pl.BlockSpec(memory_space=pl.ANY),
         out_shape=jax.ShapeDtypeStruct((n_tok, dim), BF16),
         scratch_shapes=[pltpu.VMEM((n_seq, seq_len, dim), BF16), pltpu.SemaphoreType.DMA((n_seq,)), pltpu.SemaphoreType.DMA((n_seq,))],
         name='place_sequences',
-    )(src, z)
+    )(owner, z)
 
 
 def solution(mesh):
@@ -503,30 +530,11 @@
     group_axes = ('data', 'pp')
 
     def device_step(expert_out, expert_id, slot_id, gate, resid, owner, norm_w, w_q, w_k, w_v, w_o):
-        me = lax.axis_index('ep')
-        out_local, h = expert_out[0, 0], resid[0, 0]
-        cap_dev = out_local.shape[1] // n_ep
-        n_tok = h.shape[0]
-        n_seq = owner.shape[1]
-        seq_dev = n_seq // n_ep
-        seq_len = n_tok // seq_dev
-
-        ids, slots = expert_id[0, 0].T, slot_id[0, 0].T
-        index = jnp.where(slots >= 0, ids * cap_dev + slots - me * cap_dev, -1).astype(F32)
-        table = jnp.concatenate([index, gate[0, 0].T], axis=0)
-
-        owned = owner[0].reshape(n_ep, seq_dev)
-        sender = owned // seq_dev
-        rows = jnp.arange(seq_dev)
-        second = jnp.sum((sender[:, :, None] == sender[:, None, :]) & (rows[None, :] < rows[:, None]), axis=2)
-        code = (2 * jnp.arange(n_ep)[:, None] + second).reshape(n_seq)
-        meta = jnp.sum(jnp.where(owner[0][None, :] == jnp.arange(n_seq)[:, None], code[None, :], 0), axis=1).astype(F32)
-        meta = jnp.pad(meta.reshape(n_ep, seq_dev), ((0, 8 - n_ep), (0, 128 - seq_dev)), constant_values=-1)
-
-        z = stage(out_local, table, meta, h, norm_w, w_q[0], w_k[0], w_v[0], w_o[0], seq_len, n_ep, n_stages)
-
-        src = lax.dynamic_index_in_dim(second * n_ep + sender, me, 0, keepdims=False).astype(jnp.int32)
-        return place_sequences(src, z, seq_len)[None, None]
+        n_tok = resid.shape[2]
+        seq_len = n_tok * n_ep // owner.shape[1]
+        z = stage(expert_out[0, 0], expert_id[0, 0].T, slot_id[0, 0].T, gate[0, 0].T, owner, resid[0, 0], norm_w, w_q[0], w_k[0], w_v[0], w_o[0],
+                  seq_len, n_ep, n_stages)
+        return place_sequences(owner, z, seq_len, n_ep)[None, None]
 
     tok_spec = P(group_axes, None, 'ep', None)
     weight_spec = P('pp', None, None)

time: 285 us -> 262 us (0.919)
  Pallas kernels: 279 us -> 262 us
  other arithmetic: 4.43 us -> 0 us
    pallas_call x1, Pallas kernels: 275 us -> 258 us  [stage(): pl.pallas_call(functools.partial(stage_kernel, n_ep, n_stages, dk, bn, se...]
where the time goes in v4:
time: 262 us
  Pallas kernels  262 us (100%)
    pallas_call x1, Pallas kernels, stage(): pl.pallas_call(functools.partial(stage_kernel, n_ep, n_stages, dk, bn, se...  258 us

profile of v4, /device:TPU:0, one launch (start us, length us, event | category | flops | bytes accessed | tf_op | source)
XLA Modules:
  0.0 262.1 jit_solution(18253174325814640205)
XLA Ops:
  0.0 258.3 %stage.1.z_hbm = bf16[256,7168]{1,0:T(8,128)(2,1)} custom-call(bf16[96,32,7168]{2,1,0:T(8,128)(2,1)} %bitcast.16, s32[8,256]{1,0:T(8,128)} %bitcast.18, s32[8,256]{1,0:T(8,128)} %bitcast.19, f32[8,256]{1,0:T(8,128)} %bitcast.20, s32[1,32]{1,0:T(1,128)} %own_ref.3, bf16[256,7168]{1,0:T(8,128)(2,1)} %bitcast.17, f32[1,7168]{1,0:T(1,128)} %nw_ref.1, ...), custom_call_target="tpu_custom_call" | custom-call | tf_op jit(solution)/shard_map/stage/pallas_call | solution.py:424
  258.3 3.8 %place_sequences.1 = bf16[256,7168]{1,0:T(8,128)(2,1)} custom-call(s32[1,32]{1,0:T(1,128)} %own_ref.3, bf16[256,7168]{1,0:T(8,128)(2,1)} %stage.1.z_hbm), custom_call_target="tpu_custom_call" | custom-call | tf_op jit(solution)/shard_map/place_sequences/pallas_call | solution.py:516

commit v5 on v4

--- a/solution.py
+++ b/solution.py
@@ -35,7 +35,7 @@
     width = abuf.shape[1]
     n_hp = width // bn
     n_ot = dim // bn
-    n_w, ring_z, ring_r = wbuf.shape[0], zscr.shape[0], recv_z.shape[0]
+    n_w, ring_z, ring_r, ring_o = wbuf.shape[0], zscr.shape[0], recv_z.shape[0], zout.shape[0]
     n_tile = 3 * n_hp + n_ot
 
     def col(k, w):
@@ -54,14 +54,17 @@
     def a_copy(u):
         return to_core(send_a.at[lax.rem(u, 2)], recv_a.at[lax.rem(u, ring_a)], sa_sem.at[lax.rem(u, 2)], ra_sem.at[lax.rem(u, ring_a)])
 
-    def b_copy(u):
+    halves = [slice(0, rows_g // 2), slice(rows_g // 2, rows_g)]
+
+    def b_copy(u, h):
         i = lax.rem(u, ring_b)
-        return pltpu.make_async_remote_copy(send_b.at[i], recv_b.at[i], sb_sem.at[i], rb_sem.at[i], device_id={'ep': x_peer}, device_id_type=MESH)
-
-    def c_copy(u):
+        return pltpu.make_async_remote_copy(send_b.at[i, halves[h]], recv_b.at[i, halves[h]], sb_sem.at[2 * i + h], rb_sem.at[2 * i + h],
+                                            device_id={'ep': x_peer}, device_id_type=MESH)
+
+    def c_copy(u, h):
         i = lax.rem(u, ring_c)
-        return pltpu.make_async_remote_copy(send_c.at[i], y_own.at[u // nk, :, col(lax.rem(u, nk), dk)], sc_sem.at[i], rc_sem.at[u],
-                                            device_id={'pp': other_rank}, device_id_type=MESH)
+        return pltpu.make_async_remote_copy(send_c.at[i, halves[h]], y_own.at[u // nk, halves[h], col(lax.rem(u, nk), dk)], sc_sem.at[2 * i + h],
+                                            rc_sem.at[2 * u + h], device_id={'pp': other_rank}, device_id_type=MESH)
 
     def x_copy(g, p):
         at = xbuf.at[g, pl.ds(pl.multiple_of(core * rows_g + p * 32, 32), 32)]
@@ -72,7 +75,7 @@
         return to_core(zscr.at[lax.rem(t, ring_z), theirs], recv_z.at[lax.rem(t, ring_r)], sz_sem.at[lax.rem(t, ring_z)], rz_sem.at[lax.rem(t, ring_r)])
 
     def out_copy(t):
-        i = lax.rem(t, ring_z)
+        i = lax.rem(t, ring_o)
         return pltpu.make_async_copy(zout.at[i], z_hbm.at[col(t // n_ot, rows_g), col(lax.rem(t, n_ot), bn)], out_sem.at[i])
 
     def w_slot(s):
@@ -171,7 +174,8 @@
 
         @pl.when(u >= ring_b)
         def _():
-            b_copy(u - ring_b).wait_send()
+            for h in range(2):
+                b_copy(u - ring_b, h).wait_send()
 
         for o in range(n_ep):
             @pl.when(lax.rem(u, nk) == 0)
@@ -224,18 +228,20 @@
         def _():
             pl.semaphore_wait(b_free, 1)
 
-        b_copy(u).start()
+        for h in range(2):
+            b_copy(u, h).start()
 
     def across_y(u):
         i = lax.rem(u, ring_b)
-        b_copy(u).wait_recv()
-
-        @pl.when(u >= ring_c)
-        def _():
-            c_copy(u - ring_c).wait_send()
-
-        send_c[lax.rem(u, ring_c)] = (keep[i] + recv_b[i]).astype(BF16)
-        c_copy(u).start()
+        for h in range(2):
+            b_copy(u, h).wait_recv()
+
+            @pl.when(u >= ring_c)
+            def _():
+                c_copy(u - ring_c, h).wait_send()
+
+            send_c[lax.rem(u, ring_c), halves[h]] = (keep[i, halves[h]] + recv_b[i, halves[h]]).astype(BF16)
+            c_copy(u, h).start()
 
         @pl.when(u < n_unit - ring_b)
         def _():
@@ -254,9 +260,9 @@
         def _():
             partial_sums(u)
 
-        @pl.when((u >= 2) & (u < 2 + n_w))
-        def _():
-            start_tile(u - 2)
+        @pl.when((u >= 4) & (u < 4 + n_w))
+        def _():
+            start_tile(u - 4)
 
         @pl.when(u >= 1)
         def _():
@@ -273,41 +279,54 @@
     def attend(hp):
         abuf[:, col(hp, bn)] = head_mix(head_probs(head_scores(q_scr[...], k_scr[...]), seq_len), v_scr[...])
 
-    q_scr[...] = jnp.zeros_like(q_scr)
-    k_scr[...] = jnp.zeros_like(k_scr)
-    v_scr[...] = jnp.zeros_like(v_scr)
-
-    def under(hp):
-        return (hp + 1) * 3 // 5 if isinstance(hp, int) else lax.div((hp + 1) * 3, 5)
-
-    n_last = max(0, nk - under(n_hp - 1) - (n_ot // 2 + 2) // 3)
+
+    def by_heads(hp):
+        return (hp + 1) * 9 // 16
+
+    def by_tiles(i):
+        return by_heads(n_hp - 1) + (i + 1) * 5 // (n_ot // 2)
+
+    n_last = nk - by_tiles(n_ot // 2 - 1)
+
+    def pass_on(first, last):
+        def unit(v, _):
+            across_y(nk + v)
+            return 0
+
+        lax.fori_loop(first, last, unit, 0)
+
+    def finish_waits(t):
+        z_copy(t).wait_recv()
+
+        @pl.when(t >= ring_o)
+        def _():
+            out_copy(t - ring_o).wait()
+
+    def finish_sum(t):
+        mine = pl.ds(pl.multiple_of(core * rows_g, rows_g), rows_g)
+        proj = (zscr[lax.rem(t, ring_z), mine, :] + recv_z[lax.rem(t, ring_r)]).astype(BF16)
+        zout[lax.rem(t, ring_o)] = (y_own[t // n_ot, :, col(lax.rem(t, n_ot), bn)].astype(F32) + proj.astype(F32)).astype(BF16)
+
+    def finish_starts(t):
+        out_copy(t).start()
+
+        @pl.when(t < 2 * n_ot - ring_r)
+        def _():
+            pl.semaphore_signal(z_free, inc=1, device_id={'ep': core_peer}, device_id_type=MESH)
 
     def finish(t):
-        g, i = t // n_ot, lax.rem(t, ring_z)
-        mine = pl.ds(pl.multiple_of(core * rows_g, rows_g), rows_g)
-        z_copy(t).wait_recv()
-        proj = (zscr[i, mine, :] + recv_z[lax.rem(t, ring_r)]).astype(BF16)
-
-        @pl.when(t < 2 * n_ot - ring_r)
-        def _():
-            pl.semaphore_signal(z_free, inc=1, device_id={'ep': core_peer}, device_id_type=MESH)
-
-        @pl.when(t >= ring_z)
-        def _():
-            out_copy(t - ring_z).wait()
-
-        zout[i] = (y_own[g, :, col(lax.rem(t, n_ot), bn)].astype(F32) + proj.astype(F32)).astype(BF16)
-        out_copy(t).start()
+        finish_waits(t)
+        finish_sum(t)
+        finish_starts(t)
 
     def group_pass(g, _):
-        def late(u, _):
-            across_y(u)
-            return 0
-
-        lax.fori_loop(jnp.where(g == 0, ahead, n_unit - n_last), jnp.where(g == 0, nk, n_unit), late, 0)
+        @pl.when(g == 1)
+        def _():
+            pass_on(nk - n_last, nk)
 
         def arrived(k, _):
-            c_copy(g * nk + k).wait_recv()
+            for h in range(2):
+                c_copy(g * nk + k, h).wait_recv()
             return 0
 
         lax.fori_loop(0, nk, arrived, 0)
@@ -326,7 +345,21 @@
             x_copy(g, p).wait()
             return 0
 
+        mine = pl.ds(pl.multiple_of(core * rows_g, rows_g), rows_g)
+        theirs = pl.ds(pl.multiple_of((1 - core) * rows_g, rows_g), rows_g)
+        first = g * n_tile
+
+        def project_half(rows):
+            for kind, scr in enumerate((q_scr, k_scr, v_scr)):
+                scr[rows, :] = jnp.dot(xbuf[g, rows, :], wbuf[lax.rem(first + kind, n_w)], preferred_element_type=F32).astype(BF16)
+
+        for kind in range(3):
+            qkv_tile(first + kind, 0, kind).wait()
+        project_half(mine)
         lax.fori_loop(0, rows_g // 32, exchanged, 0)
+        project_half(theirs)
+        for kind in range(3):
+            start_tile(first + kind + n_w)
 
         def heads(hp, _):
             s = g * n_tile + hp * 3
@@ -337,54 +370,56 @@
             mixed = head_mix(head_probs(scores, seq_len), v_scr[...])
             k = jnp.dot(xbuf[g], wbuf[lax.rem(s + 1, n_w)], preferred_element_type=F32).astype(BF16)
             v = jnp.dot(xbuf[g], wbuf[lax.rem(s + 2, n_w)], preferred_element_type=F32).astype(BF16)
-            abuf[:, col(jnp.maximum(hp - 1, 0), bn)] = mixed
+            abuf[:, col(hp - 1, bn)] = mixed
             q_scr[...] = q
             k_scr[...] = k
             v_scr[...] = v
             for kind in range(3):
                 start_tile(s + kind + n_w)
 
-            @pl.when((g == 0) & (under(hp) > under(hp - 1)))
-            def _():
-                across_y(nk + under(hp) - 1)
+            @pl.when(g == 0)
+            def _():
+                pass_on(jnp.where(hp == 1, 0, by_heads(hp - 1)), by_heads(hp))
 
             return 0
 
-        lax.fori_loop(0, n_hp, heads, 0)
+        lax.fori_loop(1, n_hp, heads, 0)
         attend(n_hp - 1)
 
         def project(i, _):
+            t = g * n_ot + 2 * i
+            s = g * n_tile + 3 * n_hp + 2 * i
+
+            def multiply():
+                z = [jnp.dot(abuf[...], wbuf[lax.rem(s + r, n_w), 0:width, :], preferred_element_type=F32) for r in range(2)]
+                for r in range(2):
+                    zscr[lax.rem(t + r, ring_z)] = z[r]
+
             for r in range(2):
-                t = g * n_ot + 2 * i + r
-                s = g * n_tile + 3 * n_hp + 2 * i + r
-
                 @pl.when(t >= ring_z)
                 def _():
-                    z_copy(t - ring_z).wait_send()
-
-                out_tile(s, 2 * i + r).wait()
+                    z_copy(t + r - ring_z).wait_send()
+
+                out_tile(s + r, 2 * i + r).wait()
+
+            multiply()
             for r in range(2):
-                t = g * n_ot + 2 * i + r
-                s = g * n_tile + 3 * n_hp + 2 * i + r
-                zscr[lax.rem(t, ring_z)] = jnp.dot(abuf[...], wbuf[lax.rem(s, n_w), 0:width, :], preferred_element_type=F32)
-            for r in range(2):
-                t = g * n_ot + 2 * i + r
-                start_tile(g * n_tile + 3 * n_hp + 2 * i + r + n_w)
+                start_tile(s + r + n_w)
 
                 @pl.when(t >= ring_r)
                 def _():
                     pl.semaphore_wait(z_free, 1)
 
-                z_copy(t).start()
+                z_copy(t + r).start()
 
             @pl.when(i >= 1)
             def _():
-                finish(g * n_ot + 2 * i - 2)
-                finish(g * n_ot + 2 * i - 1)
-
-            @pl.when((g == 0) & (lax.rem(i, 3) == 0) & (under(n_hp - 1) + i // 3 < nk))
-            def _():
-                across_y(nk + under(n_hp - 1) + i // 3)
+                finish(t - 2)
+                finish(t - 1)
+
+            @pl.when(g == 0)
+            def _():
+                pass_on(by_tiles(i - 1), by_tiles(i))
 
             return 0
 
@@ -401,11 +436,14 @@
     for u in range(n_unit - 2, n_unit):
         a_copy(u).wait_send()
     for u in range(n_unit - ring_b, n_unit):
-        b_copy(u).wait_send()
+        for h in range(2):
+            b_copy(u, h).wait_send()
     for u in range(n_unit - ring_c, n_unit):
-        c_copy(u).wait_send()
+        for h in range(2):
+            c_copy(u, h).wait_send()
     for t in range(2 * n_ot - ring_z, 2 * n_ot):
         z_copy(t).wait_send()
+    for t in range(2 * n_ot - ring_o, 2 * n_ot):
         out_copy(t).wait()
 
 
@@ -417,7 +455,7 @@
     width = w_q.shape[1] // 2
     rows_g = n_tok // 2
     n_unit = 2 * dim // dk
-    n_w, ring_a, ring_b, ring_c, ring_z, ring_r = 7, 3, 15, 2, 4, 4
+    n_w, ring_a, ring_b, ring_c, ring_z, ring_r, ring_o = 7, 3, 15, 2, 4, 4, 4
     any_spec = pl.BlockSpec(memory_space=pl.ANY)
     vmem_spec = pl.BlockSpec(memory_space=pltpu.VMEM)
     vmem, dma = pltpu.VMEM, pltpu.SemaphoreType.DMA
@@ -448,9 +486,9 @@
             vmem((n_tok, bn), BF16), vmem((n_tok, bn), BF16), vmem((n_tok, bn), BF16),
             vmem((ring_z, n_tok, bn), F32),
             vmem((ring_r, rows_g, bn), F32),
-            vmem((ring_z, rows_g, bn), BF16),
-            dma((n_ep,)), dma((1,)), dma((2,)), dma((ring_a,)), dma((ring_b,)), dma((ring_b,)), dma((ring_c,)), dma((n_unit,)),
-            dma((rows_g // 32,)), dma((2 * rows_g // 32,)), dma((n_w,)), dma((ring_z,)), dma((ring_r,)), dma((ring_z,)),
+            vmem((ring_o, rows_g, bn), BF16),
+            dma((n_ep,)), dma((1,)), dma((2,)), dma((ring_a,)), dma((2 * ring_b,)), dma((2 * ring_b,)), dma((2 * ring_c,)), dma((2 * n_unit,)),
+            dma((rows_g // 32,)), dma((2 * rows_g // 32,)), dma((n_w,)), dma((ring_z,)), dma((ring_r,)), dma((ring_o,)),
             dma((n_ep,)), dma((n_ep,)), dma((1,)), dma((1,)),
             pltpu.SemaphoreType.REGULAR, pltpu.SemaphoreType.REGULAR, pltpu.SemaphoreType.REGULAR,
         ],

time: 262 us -> 261 us (level)
  no operation moved by 1% of the time
where the time goes in v5:
time: 261 us
  Pallas kernels  261 us (100%)
    pallas_call x1, Pallas kernels, stage(): pl.pallas_call(functools.partial(stage_kernel, n_ep, n_stages, dk, bn, se...  257 us

profile of v5, /device:TPU:0, one launch (start us, length us, event | category | flops | bytes accessed | tf_op | source)
XLA Modules:
  0.0 261.1 jit_solution(12883650961653528761)
XLA Ops:
  0.0 257.4 %stage.1.z_hbm = bf16[256,7168]{1,0:T(8,128)(2,1)} custom-call(bf16[96,32,7168]{2,1,0:T(8,128)(2,1)} %bitcast.16, s32[8,256]{1,0:T(8,128)} %bitcast.18, s32[8,256]{1,0:T(8,128)} %bitcast.19, f32[8,256]{1,0:T(8,128)} %bitcast.20, s32[1,32]{1,0:T(1,128)} %own_ref.3, bf16[256,7168]{1,0:T(8,128)(2,1)} %bitcast.17, f32[1,7168]{1,0:T(1,128)} %nw_ref.1, ...), custom_call_target="tpu_custom_call" | custom-call | tf_op jit(solution)/shard_map/stage/pallas_call | solution.py:462
  257.4 3.8 %place_sequences.1 = bf16[256,7168]{1,0:T(8,128)(2,1)} custom-call(s32[1,32]{1,0:T(1,128)} %own_ref.3, bf16[256,7168]{1,0:T(8,128)(2,1)} %stage.1.z_hbm), custom_call_target="tpu_custom_call" | custom-call | tf_op jit(solution)/shard_map/place_sequences/pallas_call | solution.py:554
